TPU v7x, 32 devices: a whole 2x2x4 slice. The times are simulated.
32 devices in a mesh: line: 16 (over z, x, core), view: 2 (over y).
Axes of the slice: x: 2, y: 2, z: 4, core: 2. Of those that a mesh axis runs over, the one named last changes fastest.
Arguments:
- light_field: bfloat16 [16, 8, 8, 1024], P('line', None, 'view'), may hold values from -6 to 6
- query_weight: bfloat16 [2, 64, 128], replicated, may hold values from -0.75 to 0.75
- key_weight: bfloat16 [2, 64, 128], replicated, may hold values from -24 to 24
- value_weight: bfloat16 [2, 64, 128], replicated, may hold values from -0.75 to 0.75
- out_weight: bfloat16 [2, 128, 64], replicated, may hold values from -0.5 to 0.5
- conv_first: bfloat16 [3, 3, 64, 64], replicated, may hold values from -0.25 to 0.25
- conv_second: bfloat16 [3, 3, 64, 64], replicated, may hold values from -0.25 to 0.25
Outputs:
- result: bfloat16 [16, 8, 8, 1024], P('line', None, 'view')
All inputs are finite; a program needn't handle non-finite values.
Results may differ from a plain program's by a relative error of at most 0.0069.
Values may be sent and summed in bfloat16 or wider, within the bound.
No kernel may reach another device: no remote copies, remote signals or barrier semaphores. Data moves between devices by JAX's collectives and lax.ppermute only.
A program may use at most 64 MiB of HBM per device.

v0:
```python
import math

import jax
import jax.numpy as jnp
from jax import lax
from jax.sharding import PartitionSpec as P


def padded_2(block, sides, width):
    for axis, dim in sides:
        count = lax.axis_size(axis)
        forward = [(i, i + 1) for i in range(count - 1)]
        backward = [(target, source) for source, target in forward]
        low = lax.ppermute(
            lax.slice_in_dim(block, block.shape[dim] - width, None, axis=dim), axis, forward
        )
        high = lax.ppermute(lax.slice_in_dim(block, 0, width, axis=dim), axis, backward)
        block = jnp.concatenate([low, block, high], axis=dim)
    return block


def layer_norm(tokens):
    values = tokens.astype(jnp.float32)
    centre = values - jnp.mean(values, axis=-1, keepdims=True)
    spread = jnp.mean(centre * centre, axis=-1, keepdims=True)
    return (centre * lax.rsqrt(spread + 1e-05)).astype(jnp.bfloat16)


def project(inputs, matrix):
    return jnp.dot(inputs, matrix, preferred_element_type=jnp.float32).astype(jnp.bfloat16)


def attend(tokens, query_matrix, key_matrix, value_matrix, out_matrix):
    normed = layer_norm(tokens)
    queries = project(normed, query_matrix)
    keys = project(normed, key_matrix)
    values = project(normed, value_matrix)
    line_count, token_count, att_width = queries.shape
    block_rows = math.gcd(token_count, 512)
    block_count = token_count // block_rows
    grouped = queries.reshape(line_count, block_count, block_rows, att_width)
    scaling = 1.0 / math.sqrt(att_width)

    def per_line(operands):
        query_rows, key_rows, value_rows = operands

        def per_block(query_block):
            scores = (
                jnp.einsum("qa,ka->qk", query_block, key_rows, preferred_element_type=jnp.float32)
                * scaling
            )
            exponent = jnp.exp(scores - jnp.max(scores, axis=-1, keepdims=True))
            weights = (exponent / jnp.sum(exponent, axis=-1, keepdims=True)).astype(jnp.bfloat16)
            return jnp.dot(weights, value_rows, preferred_element_type=jnp.float32).astype(
                jnp.bfloat16
            )

        return lax.map(per_block, query_rows)

    mixed = lax.map(per_line, (grouped, keys, values)).reshape(line_count, token_count, att_width)
    summed = tokens.astype(jnp.float32) + jnp.dot(
        mixed, out_matrix, preferred_element_type=jnp.float32
    )
    return summed.astype(jnp.bfloat16)


def local_correlate(edged, kernel):
    inner_rows = edged.shape[2] - 2
    column_count = edged.shape[3]
    padded = jnp.pad(edged, ((0, 0), (0, 0), (0, 0), (1, 1), (0, 0)))
    summed = jnp.zeros(edged.shape[:2] + (inner_rows, column_count, kernel.shape[3]), jnp.float32)
    for row_shift in range(3):
        for col_shift in range(3):
            window = padded[
                :, :, row_shift : row_shift + inner_rows, col_shift : col_shift + column_count, :
            ]
            summed = summed + jnp.dot(
                window, kernel[row_shift, col_shift], preferred_element_type=jnp.float32
            )
    return summed


def leaky_relu(values):
    return jnp.where(values >= 0, values, 0.1 * values)


def local(light_field, query_weight, key_weight, value_weight, out_weight, conv_first, conv_second):
    span_rows, all_u, local_v, packed = light_field.shape
    channels = query_weight.shape[1]
    columns = packed // channels
    ray_grid = light_field.reshape(span_rows, all_u, local_v, columns, channels)
    horizontal = ray_grid.transpose(0, 2, 1, 3, 4).reshape(
        span_rows * local_v, all_u * columns, channels
    )
    after_rows = attend(horizontal, query_weight[0], key_weight[0], value_weight[0], out_weight[0])
    leaving = after_rows.reshape(span_rows, local_v, all_u, columns, channels).transpose(
        3, 0, 1, 2, 4
    )
    leaving = leaving.reshape(columns, span_rows, local_v, all_u * channels)
    arrived = lax.all_to_all(
        lax.all_to_all(leaving, "line", split_axis=0, concat_axis=1, tiled=True),
        "view",
        split_axis=3,
        concat_axis=2,
        tiled=True,
    )
    local_cols, all_rows, all_v, packed_u = arrived.shape
    local_u = packed_u // channels
    vertical = arrived.reshape(local_cols, all_rows, all_v, local_u, channels).transpose(
        3, 0, 2, 1, 4
    )
    vertical = vertical.reshape(local_u * local_cols, all_v * all_rows, channels)
    second = attend(vertical, query_weight[1], key_weight[1], value_weight[1], out_weight[1])
    outgoing = second.reshape(local_u, local_cols, all_v, all_rows, channels).transpose(
        1, 3, 2, 0, 4
    )
    outgoing = outgoing.reshape(local_cols, all_rows, all_v, local_u * channels)
    padded_rows = jnp.pad(outgoing, ((0, 0), (1, 1), (0, 0), (0, 0)))
    lower_rim = padded_rows[:, 0:all_rows:span_rows]
    upper_rim = padded_rows[:, span_rows + 1 :: span_rows]
    inner = padded_rows[:, 1 : all_rows + 1].reshape(
        local_cols, all_rows // span_rows, span_rows, all_v, local_u * channels
    )
    framed = jnp.concatenate((lower_rim[:, :, None], inner, upper_rim[:, :, None]), axis=2)
    framed = framed.reshape(
        local_cols, all_rows // span_rows * (span_rows + 2), all_v, local_u * channels
    )
    returned = lax.all_to_all(
        lax.all_to_all(framed, "line", split_axis=1, concat_axis=0, tiled=True),
        "view",
        split_axis=2,
        concat_axis=3,
        tiled=True,
    )
    edged = returned.reshape(columns, span_rows + 2, local_v, all_u, channels).transpose(
        3, 2, 1, 0, 4
    )
    restored = edged[:, :, 1 : span_rows + 1]
    hidden = leaky_relu(local_correlate(edged, conv_first)).astype(jnp.bfloat16)
    hidden_edged = padded_2(
        hidden.reshape(all_u, local_v, span_rows, columns * channels), (("line", 2),), 1
    )
    hidden_edged = hidden_edged.reshape(all_u, local_v, span_rows + 2, columns, channels)
    summed = restored.astype(jnp.float32) + local_correlate(hidden_edged, conv_second)
    result = summed.astype(jnp.bfloat16).transpose(2, 0, 1, 3, 4)
    return result.reshape(span_rows, all_u, local_v, columns * channels)


def solution(mesh):
    placed = (P("line", None, "view", None), P(), P(), P(), P(), P(), P())
    return jax.shard_map(
        local, mesh=mesh, in_specs=placed, out_specs=P("line", None, "view", None), check_vma=False
    )
```

profile of v0, /device:TPU:3, one launch (start us, length us, event | category | flops | bytes accessed | tf_op | source)
XLA Modules:
  0.0 64.1 jit_solution(3023901769148771560)
XLA Ops:
  0.0 1.0 %reshape.271 = f32[1,8,4,16,64]{4,3,2,1,0:T(8,128)S(1)} reshape(bf16[1,8,4,1024]{3,2,1,0:T(4,128)(2,1)} %param.11) | data formatting | bytes 196608 | tf_op jit(solution)/shard_map/convert_element_type | solution.py:61
  1.2 0.3 multiply_reduce_fusion.1
  1.5 0.2 multiply_convert_fusion.1
  1.7 0.2 copy-done.2
  2.4 1.8 %while.20 = (s32[]{:T(128)}, bf16[4,1,128,128]{3,2,1,0:T(8,128)(2,1)S(1)}, bf16[4,1,128,128]{3,2,1,0:T(8,128)(2,1)S(1)}, bf16[4,128,128]{2,1,0:T(8,128)(2,1)S(1)}, bf16[4,128,128]{2,1,0:T(8,128)(2,1)S(1)}, /*index=5*/s32[]{:T(128)}) while((s32[]{:T(128)}, bf16[4,1,128,128]{3,2,1,0:T(8,128)(2,1)S(1)}, bf16[4,1,128,128]{3,2,1,0:T(8,128)(2,1)S(1)}, ...), condition=%wide.region_5.6_spmd, body=%wide.region_2.5_spmd.sunk | while | flops 8519426 | bytes 332357 | solution.py:60
  2.4 0.2 fusion.142
  2.7 0.2 fusion.144
  2.9 0.2 fusion.142
  3.1 0.2 fusion.144
  3.4 0.2 fusion.142
  3.6 0.2 fusion.144
  3.8 0.2 fusion.142
  4.0 0.2 fusion.144
  4.4 0.2 fusion.33
  4.9 11.5 %all_to_all.51 = bf16[16,1,4,512]{3,2,1,0:T(4,128)(2,1)S(1)} all-to-all(bf16[16,1,4,512]{3,2,1,0:T(4,128)(2,1)S(1)} %reshape.301), channel_id=1, replica_groups=mesh['line'=16,'view'=2] {'line'}, dimensions={0} | all-to-all | bytes 131072 | tf_op jit(solution)/shard_map/all_to_all | solution.py:101
  16.4 0.3 copy.123
  16.7 0.5 reshape.302
  17.3 5.3 %all_to_all.52 = bf16[2,2,8192]{2,1,0:T(2,128)(2,1)S(1)} all-to-all(bf16[2,2,8192]{2,1,0:T(2,128)(2,1)S(1)} %reshape.302), channel_id=1, replica_groups=mesh['line'=16,'view'=2] {'view'}, dimensions={0} | all-to-all | bytes 131072 | tf_op jit(solution)/shard_map/all_to_all | solution.py:100
  22.6 0.4 reshape.303
  23.0 0.3 copy.124
  23.6 0.2 bitcast_reduce_fusion
  24.0 0.4 multiply_reduce_fusion
  24.7 0.3 multiply_convert_fusion
  25.6 1.8 %while.21 = (s32[]{:T(128)}, bf16[4,1,128,128]{3,2,1,0:T(8,128)(2,1)S(1)}, bf16[4,1,128,128]{3,2,1,0:T(8,128)(2,1)S(1)}, bf16[4,128,128]{2,1,0:T(8,128)(2,1)S(1)}, bf16[4,128,128]{2,1,0:T(8,128)(2,1)S(1)}, /*index=5*/s32[]{:T(128)}) while((s32[]{:T(128)}, bf16[4,1,128,128]{3,2,1,0:T(8,128)(2,1)S(1)}, ...), condition=%wide.region_11.12_spmd, body=%wide.region_8.11_spmd.sunk | while | flops 8519426 | bytes 332357 | solution.py:60
  25.6 0.2 fusion.146
  25.8 0.2 fusion.148
  26.1 0.2 fusion.146
  26.3 0.2 fusion.148
  26.5 0.2 fusion.146
  26.7 0.2 fusion.148
  27.0 0.2 fusion.146
  27.2 0.2 fusion.148
  27.5 0.2 fusion.34
  28.3 12.9 %all_to_all.53 = bf16[1,48,8,256]{3,2,0,1:T(8,128)(2,1)S(1)} all-to-all(bf16[1,48,8,256]{3,2,0,1:T(8,128)(2,1)S(1)} %bitcast.378), channel_id=1, replica_groups=mesh['line'=16,'view'=2] {'line'}, dimensions={1} | all-to-all | bytes 393216 | tf_op jit(solution)/shard_map/all_to_all | solution.py:129
  41.3 6.8 %all_to_all.54 = bf16[16,3,8,256]{3,0,1,2:T(8,128)(2,1)S(1)} all-to-all(bf16[16,3,8,256]{3,0,1,2:T(8,128)(2,1)S(1)} %copy.142), channel_id=1, replica_groups=mesh['line'=16,'view'=2] {'view'}, dimensions={2} | all-to-all | bytes 393216 | tf_op jit(solution)/shard_map/all_to_all | solution.py:128
  48.1 0.2 copy.144
  48.3 0.3 reshape.248
  48.7 0.5 copy-done
  49.5 0.2 convolution_add_fusion.13
  49.7 0.2 convolution_add_fusion.12
  50.2 0.2 convolution_add_fusion.9
  50.6 0.2 fusion.62
  51.0 3.6 %collective-permute-start = (bf16[8,4,1,1024]{3,1,0,2:T(4,128)(2,1)S(1)}, bf16[8,4,1,1024]{3,1,0,2:T(4,128)(2,1)S(1)}, u32[]{:S(2)}, u32[]{:S(2)}) collective-permute-start(bf16[8,4,1,1024]{3,1,0,2:T(4,128)(2,1)S(1)} %reshape.258), channel_id=1, source_target_pairs={{0,2},{2,4},{4,6},{6,8},{8,10},{10,12},{12,14},{14,16},{16,18},{18... | collective-permute-start | bytes 196616 | tf_op jit(solution)/shard_map/ppermute | solution.py:14
  54.6 1.9 %collective-permute-start.1 = (bf16[8,4,1,1024]{3,1,0,2:T(4,128)(2,1)S(1)}, bf16[8,4,1,1024]{3,1,0,2:T(4,128)(2,1)S(1)}, u32[]{:S(2)}, u32[]{:S(2)}) collective-permute-start(bf16[8,4,1,1024]{3,1,0,2:T(4,128)(2,1)S(1)} %reshape.258), channel_id=1, source_target_pairs={{2,0},{4,2},{6,4},{8,6},{10,8},{12,10},{14,12},{16,14},{18,16},{20... | collective-permute-start | bytes 196616 | tf_op jit(solution)/shard_map/ppermute | solution.py:17
  56.8 4.3 %collective-permute-done.1 = bf16[8,4,1,1024]{3,1,0,2:T(4,128)(2,1)S(1)} collective-permute-done((bf16[8,4,1,1024]{3,1,0,2:T(4,128)(2,1)S(1)}, bf16[8,4,1,1024]{3,1,0,2:T(4,128)(2,1)S(1)}, u32[]{:S(2)}, u32[]{:S(2)}) %collective-permute-start.1) | collective-permute-done | bytes 65568 | tf_op jit(solution)/shard_map/ppermute | solution.py:17
  61.2 0.2 fusion.39
  63.1 0.2 fusion.30
  63.3 0.8 %reshape_transpose.3 = bf16[1,8,4,1024]{3,2,1,0:T(4,128)(2,1)} reshape(bf16[8,4,1,16,64]{4,3,1,0,2:T(8,128)(2,1)S(1)} %fusion.30) | data formatting | bytes 131072 | tf_op jit(solution)/shard_map/reshape;transpose | solution.py:146
  (75 shorter events, 6.6 us)
Async XLA Ops:
  1.1 0.8 %copy-start.2 = (bf16[2,64,128]{2,1,0:T(8,128)(2,1)S(1)}, bf16[2,64,128]{2,1,0:T(8,128)(2,1)}, u32[]{:S(2)}) copy-start(bf16[2,64,128]{2,1,0:T(8,128)(2,1)} %param.14) | copy-start | bytes 98308
  1.2 0.9 %copy-start.3 = (bf16[2,64,128]{2,1,0:T(8,128)(2,1)S(1)}, bf16[2,64,128]{2,1,0:T(8,128)(2,1)}, u32[]{:S(2)}) copy-start(bf16[2,64,128]{2,1,0:T(8,128)(2,1)} %param.13) | copy-start | bytes 98308
  1.2 1.0 %copy-start.4 = (bf16[2,64,128]{2,1,0:T(8,128)(2,1)S(1)}, bf16[2,64,128]{2,1,0:T(8,128)(2,1)}, u32[]{:S(2)}) copy-start(bf16[2,64,128]{2,1,0:T(8,128)(2,1)} %param.12) | copy-start | bytes 98308
  2.4 1.9 %copy-start.5 = (bf16[2,128,64]{1,2,0:T(8,128)(2,1)S(1)}, bf16[2,128,64]{1,2,0:T(8,128)(2,1)}, u32[]{:S(2)}) copy-start(bf16[2,128,64]{1,2,0:T(8,128)(2,1)} %param.15) | copy-start | bytes 98308
  48.3 0.9 %copy-start = (bf16[3,3,64,64]{3,2,1,0:T(8,128)(2,1)S(1)}, bf16[3,3,64,64]{3,2,1,0:T(8,128)(2,1)}, u32[]{:S(2)}) copy-start(bf16[3,3,64,64]{3,2,1,0:T(8,128)(2,1)} %param.16) | copy-start | bytes 221188
  51.0 5.6 %collective-permute-start = (bf16[8,4,1,1024]{3,1,0,2:T(4,128)(2,1)S(1)}, bf16[8,4,1,1024]{3,1,0,2:T(4,128)(2,1)S(1)}, u32[]{:S(2)}, u32[]{:S(2)}) collective-permute-start(bf16[8,4,1,1024]{3,1,0,2:T(4,128)(2,1)S(1)} %reshape.258), channel_id=1, source_target_pairs={{0,2},{2,4},{4,6},{6,8},{8,10},{10,12},{12,14},{14,16},{16,18},{18... | collective-permute-start | bytes 196616 | tf_op jit(solution)/shard_map/ppermute | solution.py:14
  54.6 6.5 %collective-permute-start.1 = (bf16[8,4,1,1024]{3,1,0,2:T(4,128)(2,1)S(1)}, bf16[8,4,1,1024]{3,1,0,2:T(4,128)(2,1)S(1)}, u32[]{:S(2)}, u32[]{:S(2)}) collective-permute-start(bf16[8,4,1,1024]{3,1,0,2:T(4,128)(2,1)S(1)} %reshape.258), channel_id=1, source_target_pairs={{2,0},{4,2},{6,4},{8,6},{10,8},{12,10},{14,12},{16,14},{18,16},{20... | collective-permute-start | bytes 196616 | tf_op jit(solution)/shard_map/ppermute | solution.py:17
  56.7 4.7 %copy-start.1 = (bf16[3,3,64,64]{3,2,1,0:T(8,128)(2,1)S(1)}, bf16[3,3,64,64]{3,2,1,0:T(8,128)(2,1)}, u32[]{:S(2)}) copy-start(bf16[3,3,64,64]{3,2,1,0:T(8,128)(2,1)} %param.17) | copy-start | bytes 221188
where the time goes:
time: 64.5 us; the launch traced here: 64.1 us
  blocking collectives  36.6 us (57%)
  matrix products  7.38 us (11%)
  local copies, waits for them, and re-layouts  7.21 us (11%)
  starting transfers between devices  5.56 us (9%)
  waiting for transfers between devices  4.33 us (7%)
  other arithmetic  2.33 us (4%)
    all_to_all x1, blocking collectives, local(): lax.all_to_all(framed, 'line', split_axis=1, concat_axis=0, tiled=True)  12.9 us
    all_to_all x1, blocking collectives, local(): lax.all_to_all(leaving, 'line', split_axis=0, concat_axis=1, tiled=True)  11.5 us
    all_to_all x1, blocking collectives, local(): lax.all_to_all(lax.all_to_all(framed, 'line', split_axis=1, concat_axis=0...  6.77 us
    all_to_all x1, blocking collectives, local(): lax.all_to_all(lax.all_to_all(leaving, 'line', split_axis=0, concat_axis=...  5.35 us
    ppermute x1, waiting for transfers between devices, padded_2(): lax.ppermute(lax.slice_in_dim(block, 0, width, axis=dim), axis, backward)  4.33 us
    ppermute x1, starting transfers between devices, padded_2(): lax.ppermute(lax.slice_in_dim(block, block.shape[dim] - width, None, axis...  3.64 us
    dot_general x18, matrix products, local_correlate(): jnp.dot(window, kernel[row_shift, col_shift], preferred_element_type=jnp....  2.98 us
    ppermute x1, starting transfers between devices, padded_2(): lax.ppermute(lax.slice_in_dim(block, 0, width, axis=dim), axis, backward)  1.92 us
  transfers between devices with their start and end apart: 2, of which 1 were waited for; matrix products, arithmetic and copies ran while one was open for 0% of the time, Pallas kernels for 0%

commit v1 on v0

v1 whole, which is shorter than its diff:
```python
import functools
import math

import jax
import jax.numpy as jnp
from jax import lax
from jax.experimental import pallas as pl
from jax.experimental.pallas import tpu as pltpu
from jax.sharding import PartitionSpec as P

AXES = ("line", "view")
QUERY_BLOCK = 256
F32 = jnp.float32
BF16 = jnp.bfloat16
HALO = 2


def block_ones(lanes, channels):
    rows = lax.broadcasted_iota(jnp.int32, (lanes, lanes), 0) // channels
    cols = lax.broadcasted_iota(jnp.int32, (lanes, lanes), 1) // channels
    return jnp.where(rows == cols, 1.0 / channels, 0.0).astype(F32)


def packed_norm(tokens, channels):
    ones = block_ones(tokens.shape[-1], channels)
    mean = jnp.dot(tokens.astype(BF16), ones.astype(BF16), preferred_element_type=F32)
    centre = tokens - mean
    spread = jnp.dot(
        centre * centre, ones, precision=lax.Precision.HIGHEST, preferred_element_type=F32
    )
    return (centre * lax.rsqrt(spread + 1e-05)).astype(BF16)


def project_halves(normed, query_matrix, key_matrix, value_matrix):
    joined = jnp.concatenate([query_matrix, key_matrix, value_matrix], axis=1)
    nothing = jnp.zeros_like(joined)
    halves = []
    for parts in ([joined, nothing], [nothing, joined]):
        matrix = jnp.concatenate(parts, axis=0)
        halves.append(jnp.dot(normed, matrix, preferred_element_type=F32).astype(BF16))
    return halves


def attend_rows(queries, keys, values, scaling):
    scores = (
        lax.dot_general(queries, keys, (((1,), (1,)), ((), ())), preferred_element_type=F32)
        * scaling
    )
    exponent = jnp.exp(scores - jnp.max(scores, axis=-1, keepdims=True))
    weights = (exponent / jnp.sum(exponent, axis=-1, keepdims=True)).astype(BF16)
    return jnp.dot(weights, values, preferred_element_type=F32).astype(BF16)


def attend_line(queries, keys, values, scaling, scratch):
    tokens, width = queries.shape
    if tokens <= QUERY_BLOCK:
        return attend_rows(queries, keys, values, scaling)
    scratch[0] = queries
    scratch[1] = keys
    scratch[2] = values

    def block(index, carry):
        rows = pl.ds(pl.multiple_of(index * QUERY_BLOCK, QUERY_BLOCK), QUERY_BLOCK)
        scratch[3, rows, :] = attend_rows(scratch[0, rows, :], scratch[1], scratch[2], scaling)
        return carry

    lax.fori_loop(0, tokens // QUERY_BLOCK, block, 0)
    return scratch[3]


def out_halves(out_matrix):
    nothing = jnp.zeros_like(out_matrix)
    return jnp.concatenate(
        [
            jnp.concatenate([out_matrix, nothing], axis=1),
            jnp.concatenate([nothing, out_matrix], axis=1),
        ],
        axis=0,
    )


def rows_kernel(x_ref, wq_ref, wk_ref, wv_ref, wo_ref, o_ref, held, lines):
    all_u, local_v, packed = x_ref.shape
    channels, width = wq_ref.shape
    lanes = 2 * channels
    pairs = packed // lanes
    per_line = pairs * all_u
    scaling = 1.0 / math.sqrt(width)
    for u in range(all_u):
        rows = x_ref[u].astype(F32)
        for pair in range(pairs):
            held[pl.ds((pair * all_u + u) * local_v, local_v), :] = rows[
                :, pair * lanes : (pair + 1) * lanes
            ]
    tokens = jnp.concatenate(
        [held[pl.ds(v, per_line, stride=local_v), :] for v in range(local_v)], axis=0
    )
    normed = packed_norm(tokens, channels)
    low, high = project_halves(normed, wq_ref[...], wk_ref[...], wv_ref[...])
    out_matrix = out_halves(wo_ref[...])
    for v in range(local_v):
        span = slice(v * per_line, (v + 1) * per_line)
        both = jnp.concatenate([low[span], high[span]], axis=0)
        mixed = attend_line(
            both[:, :width], both[:, width : 2 * width], both[:, 2 * width :], scaling, lines
        )
        mixed = jnp.concatenate([mixed[:per_line], mixed[per_line:]], axis=1)
        summed = tokens[span] + jnp.dot(mixed, out_matrix, preferred_element_type=F32)
        held[pl.ds(v, per_line, stride=local_v), :] = summed
    o_ref[...] = held[...].astype(BF16).reshape(o_ref.shape)


def columns_kernel(
    x_ref, wq_ref, wk_ref, wv_ref, wo_ref, o_ref, held, lines, *, local_v, views
):
    sources, chunk, lanes = x_ref.shape
    channels, width = wq_ref.shape
    count = chunk // local_v
    per_line = sources * local_v
    scaling = 1.0 / math.sqrt(width)
    held[...] = x_ref[...].astype(F32).reshape(held.shape)
    tokens = jnp.concatenate(
        [held[pl.ds(row, sources, stride=chunk), :] for row in range(chunk)], axis=0
    )
    normed = packed_norm(tokens, channels)
    halves = project_halves(normed, wq_ref[...], wk_ref[...], wv_ref[...])
    out_matrix = out_halves(wo_ref[...])
    for line in range(count):
        span = slice(line * per_line, (line + 1) * per_line)
        mixed = [
            attend_line(
                half[span, :width],
                half[span, width : 2 * width],
                half[span, 2 * width :],
                scaling,
                lines,
            )
            for half in halves
        ]
        summed = tokens[span] + jnp.dot(
            jnp.concatenate(mixed, axis=1), out_matrix, preferred_element_type=F32
        )
        for v in range(local_v):
            held[pl.ds(line * local_v + v, sources, stride=chunk), :] = summed[
                v * sources : (v + 1) * sources
            ]
    second = held[...].astype(BF16).reshape(sources, chunk, lanes)
    window = o_ref.shape[1]
    for step in range(window):
        shift = (step - HALO) * views
        edge = abs(shift)
        if edge:
            blank = jnp.zeros((edge, chunk, lanes), BF16)
        if shift < 0:
            o_ref[:edge, step] = blank
            o_ref[edge:, step] = second[: sources - edge]
        elif shift > 0:
            o_ref[sources - edge :, step] = blank
            o_ref[: sources - edge, step] = second[edge:]
        else:
            o_ref[:, step] = second


def pair_weights(kernel):
    nothing = jnp.zeros_like(kernel[0, 0])
    parts = []
    for row in range(3):
        left, middle, right = kernel[row, 0], kernel[row, 1], kernel[row, 2]
        parts += [
            jnp.concatenate([middle, left], axis=1),
            jnp.concatenate([right, middle], axis=1),
            jnp.concatenate([nothing, right], axis=1),
            jnp.concatenate([left, nothing], axis=1),
        ]
    return jnp.concatenate(parts, axis=0)


def beside(rows, per_pair):
    blank = jnp.zeros((per_pair, rows.shape[1]), rows.dtype)
    after = jnp.concatenate([rows[per_pair:], blank], axis=0)
    before = jnp.concatenate([blank, rows[:-per_pair]], axis=0)
    lane = lax.broadcasted_iota(jnp.int32, rows.shape, 1)
    return jnp.where(lane < rows.shape[1] // 2, after, before)


def conv_kernel(x_ref, first_ref, second_ref, o_ref, *, all_rows):
    sources, window, chunk, lanes = x_ref.shape
    all_u, local_v, packed = o_ref.shape
    per_pair = all_u * local_v
    pairs = packed // lanes
    rows = sources * chunk
    images = [x_ref[:, step].reshape(rows, lanes) for step in range(window)]
    wide = [jnp.concatenate([image, beside(image, per_pair)], axis=1) for image in images]
    first = pair_weights(first_ref[...])
    here = lax.axis_index("line")
    hidden = []
    for step in range(3):
        summed = jnp.dot(
            jnp.concatenate(wide[step : step + 3], axis=1), first, preferred_element_type=F32
        )
        active = jnp.where(summed >= 0, summed, 0.1 * summed)
        row = here + (step - 1)
        inside = jnp.logical_and(row >= 0, row < all_rows)
        hidden.append(jnp.where(inside, active, 0.0).astype(BF16))
    wide = [jnp.concatenate([image, beside(image, per_pair)], axis=1) for image in hidden]
    second = pair_weights(second_ref[...])
    summed = images[HALO].astype(F32) + jnp.dot(
        jnp.concatenate(wide, axis=1), second, preferred_element_type=F32
    )
    for pair in range(pairs):
        for u in range(all_u):
            start = pair * per_pair + u * local_v
            o_ref[u, :, pair * lanes : (pair + 1) * lanes] = summed[
                start : start + local_v
            ].astype(BF16)


def local(light_field, query_weight, key_weight, value_weight, out_weight, conv_first, conv_second):
    span_rows, all_u, local_v, packed = light_field.shape
    channels, width = query_weight.shape[1:]
    lanes = 2 * channels
    lines, views = lax.axis_size("line"), lax.axis_size("view")
    devices = lines * views
    packed_lines = packed // lanes * all_u
    if span_rows != 1 or packed_lines % devices:
        raise ValueError("unsupported split")
    chunk = packed_lines // devices * local_v

    weights = [
        (query_weight[i], key_weight[i], value_weight[i], out_weight[i]) for i in range(2)
    ]

    def scratch(rows, tokens):
        kept = tokens if tokens > QUERY_BLOCK else 16
        return [pltpu.VMEM((rows, lanes), F32), pltpu.VMEM((4, kept, width), BF16)]

    rows = packed_lines * local_v
    leaving = pl.pallas_call(
        rows_kernel,
        out_shape=jax.ShapeDtypeStruct((devices, chunk, lanes), BF16),
        scratch_shapes=scratch(rows, 2 * packed_lines),
        name="rows",
    )(light_field[0], *weights[0])
    arrived = lax.all_to_all(leaving, AXES, split_axis=0, concat_axis=0, tiled=True)
    window = 2 * HALO + 1
    framed = pl.pallas_call(
        functools.partial(columns_kernel, local_v=local_v, views=views),
        out_shape=jax.ShapeDtypeStruct((devices, window, chunk, lanes), BF16),
        scratch_shapes=scratch(devices * chunk, devices * local_v),
        name="columns",
    )(arrived, *weights[1])
    returned = lax.all_to_all(framed, AXES, split_axis=0, concat_axis=0, tiled=True)
    result = pl.pallas_call(
        functools.partial(conv_kernel, all_rows=lines * span_rows),
        out_shape=jax.ShapeDtypeStruct((all_u, local_v, packed), BF16),
        name="convs",
    )(returned, conv_first, conv_second)
    return result[None]


def solution(mesh):
    placed = (P("line", None, "view", None), P(), P(), P(), P(), P(), P())
    return jax.shard_map(
        local, mesh=mesh, in_specs=placed, out_specs=P("line", None, "view", None), check_vma=False
    )
```

time: 64.5 us -> 42.8 us (0.66)
  the two profiles are of different devices: /device:TPU:3 before, /device:TPU:0 now
where the time goes in v1:
time: 42.8 us; the launch traced here: 42.3 us
  blocking collectives  15 us (35%)
  Pallas kernels  9.04 us (21%)
  starting transfers between devices  7.33 us (17%)
  waiting for transfers between devices  6.89 us (16%)
  local copies, waits for them, and re-layouts  4.08 us (10%)
    all_to_all x1, blocking collectives, local(): lax.all_to_all(framed, AXES, split_axis=0, concat_axis=0, tiled=True)  15 us
    all_to_all x1, starting transfers between devices, local(): lax.all_to_all(leaving, AXES, split_axis=0, concat_axis=0, tiled=True)  7.33 us
    all_to_all x1, waiting for transfers between devices, local(): lax.all_to_all(leaving, AXES, split_axis=0, concat_axis=0, tiled=True)  6.89 us
    pallas_call x1, Pallas kernels, local(): pl.pallas_call(rows_kernel, out_shape=jax.ShapeDtypeStruct((devices, chun...  3.37 us
    pallas_call x1, Pallas kernels, local(): pl.pallas_call(functools.partial(columns_kernel, local_v=local_v, views=v...  3.28 us
    pallas_call x1, Pallas kernels, local(): pl.pallas_call(functools.partial(conv_kernel, all_rows=lines * span_rows)...  2.39 us
    unnamed x10, local copies, waits for them, and re-layouts  2.11 us
    squeeze x1, local copies, waits for them, and re-layouts, local(): query_weight[i]  1.35 us
  transfers between devices with their start and end apart: 1, of which 1 were waited for; matrix products, arithmetic and copies ran while one was open for 2% of the time, Pallas kernels for 0%

profile of v1, /device:TPU:0, one launch (start us, length us, event | category | flops | bytes accessed | tf_op | source)
XLA Modules:
  0.0 42.3 jit_solution(10958569545566592169)
XLA Ops:
  0.0 0.0 copy-start.1
  0.0 1.4 %slice_bitcast_fusion.2 = (bf16[64,128]{1,0:T(8,128)(2,1)}, bf16[64,128]{1,0:T(8,128)(2,1)}) fusion(bf16[2,64,128]{2,1,0:T(8,128)(2,1)} %param.8), kind=kLoop, calls=%fused_computation.2 | loop fusion | bytes 65536 | tf_op jit(solution)/shard_map/squeeze | solution.py:230
  1.4 0.0 copy-done.1
  1.4 0.0 copy-start.3
  1.4 0.0 copy-start.2
  1.4 0.7 %copy.10 = bf16[1,128,64]{2,1,0:T(8,128)(2,1)} copy(bf16[1,128,64]{1,2,0:T(8,128)(2,1)S(1)} %get-tuple-element.6) | data formatting | bytes 32768
  2.1 0.0 copy-done.3
  2.1 0.0 copy-done.2
  2.1 0.6 %slice_bitcast_fusion = (bf16[64,128]{1,0:T(8,128)(2,1)}, bf16[64,128]{1,0:T(8,128)(2,1)}, bf16[64,128]{1,0:T(8,128)(2,1)}, bf16[64,128]{1,0:T(8,128)(2,1)}) fusion(bf16[2,64,128]{2,1,0:T(8,128)(2,1)S(1)} %copy-done.2, bf16[2,64,128]{2,1,0:T(8,128)(2,1)S(1)} %copy-done.3), kind=kLoop, calls=%fused_computation | loop fusion | bytes 131072 | tf_op jit(solution)/shard_map/squeeze | solution.py:230
  2.8 3.4 %rows.1 = bf16[32,8,128]{2,1,0:T(8,128)(2,1)} custom-call(bf16[8,4,1024]{2,1,0:T(4,128)(2,1)} %bitcast.18, bf16[64,128]{1,0:T(8,128)(2,1)} %get-tuple-element.12.wq_ref, bf16[64,128]{1,0:T(8,128)(2,1)} %get-tuple-element.13.wk_ref, bf16[64,128]{1,0:T(8,128)(2,1)} %get-tuple-element.8.wv_ref, bf16[128,64]{1,0:T(8,128)(2,1)} %bitcast.16), custom_call_target="tpu_custom_call" | custom-call | tf_op jit(solution)/shard_map/rows/pallas_call | solution.py:238
  6.1 7.3 %all-to-all-start = ((bf16[32,8,128]{2,1,0:T(8,128)(2,1)}), bf16[32,8,128]{2,1,0:T(8,128)(2,1)S(1)}, u32[]{:S(2)}, u32[]{:S(2)}) async-start(bf16[32,8,128]{2,1,0:T(8,128)(2,1)} %rows.1), calls=%async_computation | async-start | bytes 131072 | tf_op jit(solution)/shard_map/all_to_all | solution.py:244
  13.5 0.7 %copy.11 = bf16[1,128,64]{2,1,0:T(8,128)(2,1)} copy(bf16[1,128,64]{1,2,0:T(8,128)(2,1)S(1)} %get-tuple-element.5) | data formatting | bytes 32768
  14.2 6.9 %all-to-all-done.x_ref = bf16[32,8,128]{2,1,0:T(8,128)(2,1)S(1)} async-done(((bf16[32,8,128]{2,1,0:T(8,128)(2,1)}), bf16[32,8,128]{2,1,0:T(8,128)(2,1)S(1)}, u32[]{:S(2)}, u32[]{:S(2)}) %all-to-all-start) | async-done | bytes 65568 | tf_op jit(solution)/shard_map/all_to_all | solution.py:244
  21.1 0.0 copy-start
  21.1 0.6 %copy-done = bf16[32,8,128]{2,1,0:T(8,128)(2,1)} copy-done((bf16[32,8,128]{2,1,0:T(8,128)(2,1)}, bf16[32,8,128]{2,1,0:T(8,128)(2,1)S(1)}, u32[]{:S(2)}) %copy-start) | copy-done | bytes 65560
  21.7 3.3 %columns.1 = bf16[32,5,8,128]{3,2,1,0:T(8,128)(2,1)} custom-call(bf16[32,8,128]{2,1,0:T(8,128)(2,1)} %copy-done, bf16[64,128]{1,0:T(8,128)(2,1)} %get-tuple-element.11.wq_ref, bf16[64,128]{1,0:T(8,128)(2,1)} %get-tuple-element.14.wk_ref, bf16[64,128]{1,0:T(8,128)(2,1)} %get-tuple-element.7.wv_ref, bf16[128,64]{1,0:T(8,128)(2,1)} %bitcast.17), custom_call_target="tpu_custom_call" | custom-call | tf_op jit(solution)/shard_map/columns/pallas_call | solution.py:246
  25.0 15.0 %all_to_all.10.x_ref = bf16[32,5,8,128]{3,2,1,0:T(8,128)(2,1)} all-to-all(bf16[32,5,8,128]{3,2,1,0:T(8,128)(2,1)} %columns.1), channel_id=1, replica_groups=mesh['line'=16,'view'=2] {'line','view'}, dimensions={0} | all-to-all | bytes 655360 | tf_op jit(solution)/shard_map/all_to_all | solution.py:252
  40.0 2.4 %convs.1 = bf16[8,4,1024]{2,1,0:T(4,128)(2,1)} custom-call(bf16[32,5,8,128]{3,2,1,0:T(8,128)(2,1)} %all_to_all.10.x_ref, bf16[3,3,64,64]{3,2,1,0:T(8,128)(2,1)} %first_ref.1, bf16[3,3,64,64]{3,2,1,0:T(8,128)(2,1)} %second_ref.1), custom_call_target="tpu_custom_call" | custom-call | tf_op jit(solution)/shard_map/convs/pallas_call | solution.py:253
  (1 shorter events, 0.0 us)
Async XLA Ops:
  0.0 1.4 %copy-start.1 = (bf16[2,128,64]{1,2,0:T(8,128)(2,1)S(1)}, bf16[2,128,64]{1,2,0:T(8,128)(2,1)}, u32[]{:S(2)}) copy-start(bf16[2,128,64]{1,2,0:T(8,128)(2,1)} %param.11) | copy-start | bytes 98308
  1.4 0.8 %copy-start.3 = (bf16[2,64,128]{2,1,0:T(8,128)(2,1)S(1)}, bf16[2,64,128]{2,1,0:T(8,128)(2,1)}, u32[]{:S(2)}) copy-start(bf16[2,64,128]{2,1,0:T(8,128)(2,1)} %param.9) | copy-start | bytes 98308
  1.4 0.8 %copy-start.2 = (bf16[2,64,128]{2,1,0:T(8,128)(2,1)S(1)}, bf16[2,64,128]{2,1,0:T(8,128)(2,1)}, u32[]{:S(2)}) copy-start(bf16[2,64,128]{2,1,0:T(8,128)(2,1)} %param.10) | copy-start | bytes 98308
  6.1 14.9 %all-to-all-start = ((bf16[32,8,128]{2,1,0:T(8,128)(2,1)}), bf16[32,8,128]{2,1,0:T(8,128)(2,1)S(1)}, u32[]{:S(2)}, u32[]{:S(2)}) async-start(bf16[32,8,128]{2,1,0:T(8,128)(2,1)} %rows.1), calls=%async_computation | async-start | bytes 131072 | tf_op jit(solution)/shard_map/all_to_all | solution.py:244
  21.1 0.6 %copy-start = (bf16[32,8,128]{2,1,0:T(8,128)(2,1)}, bf16[32,8,128]{2,1,0:T(8,128)(2,1)S(1)}, u32[]{:S(2)}) copy-start(bf16[32,8,128]{2,1,0:T(8,128)(2,1)S(1)} %all-to-all-done.x_ref) | copy-start | bytes 196612

commit v2 on v1

--- a/solution.py
+++ b/solution.py
@@ -13,6 +13,7 @@
 F32 = jnp.float32
 BF16 = jnp.bfloat16
 HALO = 2
+VMEM_BYTES = 16 * 1024 * 1024
 
 
 def block_ones(lanes, channels):
@@ -68,18 +69,42 @@
     return scratch[3]
 
 
-def out_halves(out_matrix):
-    nothing = jnp.zeros_like(out_matrix)
+def out_halves(flipped):
+    nothing = jnp.zeros_like(flipped)
     return jnp.concatenate(
         [
-            jnp.concatenate([out_matrix, nothing], axis=1),
-            jnp.concatenate([nothing, out_matrix], axis=1),
+            jnp.concatenate([flipped, nothing], axis=1),
+            jnp.concatenate([nothing, flipped], axis=1),
         ],
         axis=0,
     )
 
 
-def rows_kernel(x_ref, wq_ref, wk_ref, wv_ref, wo_ref, o_ref, held, lines):
+def project_out(mixed, out_matrix):
+    return lax.dot_general(
+        mixed, out_matrix, (((1,), (1,)), ((), ())), preferred_element_type=F32
+    )
+
+
+def rows_kernel(
+    x_hbm, wq_hbm, wk_hbm, wv_hbm, wo_hbm, o_ref, held, lines, x_ref, wq_ref, wk_ref, wv_ref,
+    wo_ref, arrivals,
+):
+    copies = [
+        pltpu.make_async_copy(source.at[0], target, arrivals.at[index])
+        for index, (source, target) in enumerate(
+            [
+                (x_hbm, x_ref),
+                (wq_hbm, wq_ref),
+                (wk_hbm, wk_ref),
+                (wv_hbm, wv_ref),
+                (wo_hbm, wo_ref),
+            ]
+        )
+    ]
+    for copy in copies:
+        copy.start()
+    copies[0].wait()
     all_u, local_v, packed = x_ref.shape
     channels, width = wq_ref.shape
     lanes = 2 * channels
@@ -96,6 +121,8 @@
         [held[pl.ds(v, per_line, stride=local_v), :] for v in range(local_v)], axis=0
     )
     normed = packed_norm(tokens, channels)
+    for copy in copies[1:]:
+        copy.wait()
     low, high = project_halves(normed, wq_ref[...], wk_ref[...], wv_ref[...])
     out_matrix = out_halves(wo_ref[...])
     for v in range(local_v):
@@ -105,7 +132,7 @@
             both[:, :width], both[:, width : 2 * width], both[:, 2 * width :], scaling, lines
         )
         mixed = jnp.concatenate([mixed[:per_line], mixed[per_line:]], axis=1)
-        summed = tokens[span] + jnp.dot(mixed, out_matrix, preferred_element_type=F32)
+        summed = tokens[span] + project_out(mixed, out_matrix)
         held[pl.ds(v, per_line, stride=local_v), :] = summed
     o_ref[...] = held[...].astype(BF16).reshape(o_ref.shape)
 
@@ -114,7 +141,7 @@
     x_ref, wq_ref, wk_ref, wv_ref, wo_ref, o_ref, held, lines, *, local_v, views
 ):
     sources, chunk, lanes = x_ref.shape
-    channels, width = wq_ref.shape
+    channels, width = wq_ref.shape[1:]
     count = chunk // local_v
     per_line = sources * local_v
     scaling = 1.0 / math.sqrt(width)
@@ -123,8 +150,8 @@
         [held[pl.ds(row, sources, stride=chunk), :] for row in range(chunk)], axis=0
     )
     normed = packed_norm(tokens, channels)
-    halves = project_halves(normed, wq_ref[...], wk_ref[...], wv_ref[...])
-    out_matrix = out_halves(wo_ref[...])
+    halves = project_halves(normed, wq_ref[1], wk_ref[1], wv_ref[1])
+    out_matrix = out_halves(wo_ref[1])
     for line in range(count):
         span = slice(line * per_line, (line + 1) * per_line)
         mixed = [
@@ -137,9 +164,7 @@
             )
             for half in halves
         ]
-        summed = tokens[span] + jnp.dot(
-            jnp.concatenate(mixed, axis=1), out_matrix, preferred_element_type=F32
-        )
+        summed = tokens[span] + project_out(jnp.concatenate(mixed, axis=1), out_matrix)
         for v in range(local_v):
             held[pl.ds(line * local_v + v, sources, stride=chunk), :] = summed[
                 v * sources : (v + 1) * sources
@@ -226,9 +251,8 @@
         raise ValueError("unsupported split")
     chunk = packed_lines // devices * local_v
 
-    weights = [
-        (query_weight[i], key_weight[i], value_weight[i], out_weight[i]) for i in range(2)
-    ]
+    weights = (query_weight, key_weight, value_weight, out_weight.transpose(0, 2, 1))
+    params = pltpu.CompilerParams(vmem_limit_bytes=VMEM_BYTES)
 
     def scratch(rows, tokens):
         kept = tokens if tokens > QUERY_BLOCK else 16
@@ -238,21 +262,30 @@
     leaving = pl.pallas_call(
         rows_kernel,
         out_shape=jax.ShapeDtypeStruct((devices, chunk, lanes), BF16),
-        scratch_shapes=scratch(rows, 2 * packed_lines),
+        in_specs=[pl.BlockSpec(memory_space=pltpu.HBM)] * 5,
+        scratch_shapes=scratch(rows, 2 * packed_lines)
+        + [
+            pltpu.VMEM((all_u, local_v, packed), BF16),
+            *[pltpu.VMEM((channels, width), BF16)] * 4,
+            pltpu.SemaphoreType.DMA((5,)),
+        ],
+        compiler_params=params,
         name="rows",
-    )(light_field[0], *weights[0])
+    )(*(pltpu.with_memory_space_constraint(a, pltpu.HBM) for a in (light_field, *weights)))
     arrived = lax.all_to_all(leaving, AXES, split_axis=0, concat_axis=0, tiled=True)
     window = 2 * HALO + 1
     framed = pl.pallas_call(
         functools.partial(columns_kernel, local_v=local_v, views=views),
         out_shape=jax.ShapeDtypeStruct((devices, window, chunk, lanes), BF16),
         scratch_shapes=scratch(devices * chunk, devices * local_v),
+        compiler_params=params,
         name="columns",
-    )(arrived, *weights[1])
+    )(arrived, *weights)
     returned = lax.all_to_all(framed, AXES, split_axis=0, concat_axis=0, tiled=True)
     result = pl.pallas_call(
         functools.partial(conv_kernel, all_rows=lines * span_rows),
         out_shape=jax.ShapeDtypeStruct((all_u, local_v, packed), BF16),
+        compiler_params=params,
         name="convs",
     )(returned, conv_first, conv_second)
     return result[None]

time: 42.8 us -> 34.7 us (0.81)
  blocking collectives: 15 us -> 28.3 us
  starting transfers between devices: 7.33 us -> 0 us
  waiting for transfers between devices: 6.89 us -> 0 us
  local copies, waits for them, and re-layouts: 4.08 us -> 0.04 us
  Pallas kernels: 9.04 us -> 6.01 us
    all_to_all x0 -> x1, blocking collectives: none -> 14.7 us  [local(): lax.all_to_all(leaving, AXES, split_axis=0, concat_axis=0, tiled=True)]
    all_to_all x1 -> x0, starting transfers between devices: 7.33 us -> none  [local(): lax.all_to_all(leaving, AXES, split_axis=0, concat_axis=0, tiled=True)]
    all_to_all x1 -> x0, waiting for transfers between devices: 6.89 us -> none  [local(): lax.all_to_all(leaving, AXES, split_axis=0, concat_axis=0, tiled=True)]
    unnamed x10 -> x12, local copies, waits for them, and re-layouts: 2.11 us -> 0.04 us
    squeeze x2 -> x0, local copies, waits for them, and re-layouts: 1.97 us -> none  [the longest x1 1.35 us: local(): query_weight[i]]
    pallas_call x1, Pallas kernels: 3.28 us -> 1.73 us  [local(): pl.pallas_call(functools.partial(columns_kernel, local_v=local_v, views=v...]
    all_to_all x1, blocking collectives: 15 us -> 13.5 us  [local(): lax.all_to_all(framed, AXES, split_axis=0, concat_axis=0, tiled=True)]
    pallas_call x1, Pallas kernels: 2.39 us -> 1.32 us  [local(): pl.pallas_call(functools.partial(conv_kernel, all_rows=lines * span_rows)...]
  transfers between devices with their start and end apart: 1 -> 0, of which waited for: 1 -> 0; matrix products, arithmetic and copies ran while one was open for 2% -> 0% of each run, Pallas kernels for 0% -> 0%
where the time goes in v2:
time: 34.7 us; the launch traced here: 34.4 us
  blocking collectives  28.3 us (82%)
  Pallas kernels  6.01 us (17%)
    all_to_all x1, blocking collectives, local(): lax.all_to_all(leaving, AXES, split_axis=0, concat_axis=0, tiled=True)  14.7 us
    all_to_all x1, blocking collectives, local(): lax.all_to_all(framed, AXES, split_axis=0, concat_axis=0, tiled=True)  13.5 us
    pallas_call x1, Pallas kernels, local(): pl.pallas_call(rows_kernel, out_shape=jax.ShapeDtypeStruct((devices, chun...  2.96 us
    pallas_call x1, Pallas kernels, local(): pl.pallas_call(functools.partial(columns_kernel, local_v=local_v, views=v...  1.73 us
    pallas_call x1, Pallas kernels, local(): pl.pallas_call(functools.partial(conv_kernel, all_rows=lines * span_rows)...  1.32 us

profile of v2, /device:TPU:0, one launch (start us, length us, event | category | flops | bytes accessed | tf_op | source)
XLA Modules:
  0.0 34.4 jit_solution(5405232309697485567)
XLA Ops:
  0.0 3.0 %rows.1 = bf16[32,8,128]{2,1,0:T(8,128)(2,1)S(1)} custom-call(bf16[1,8,4,1024]{3,2,1,0:T(4,128)(2,1)} %x_hbm.1, bf16[2,64,128]{2,1,0:T(8,128)(2,1)} %wq_ref.1, bf16[2,64,128]{2,1,0:T(8,128)(2,1)} %wk_ref.1, bf16[2,64,128]{2,1,0:T(8,128)(2,1)} %wv_ref.1, bf16[2,64,128]{2,1,0:T(8,128)(2,1)} %bitcast.2), custom_call_target="tpu_custom_call" | custom-call | tf_op jit(solution)/shard_map/rows/pallas_call | solution.py:262
  3.0 0.0 copy-start.2
  3.0 0.0 copy-start.3
  3.0 0.0 copy-start.4
  3.0 0.0 copy-start.5
  3.0 14.7 %all_to_all.10.x_ref = bf16[32,8,128]{2,1,0:T(8,128)(2,1)S(1)} all-to-all(bf16[32,8,128]{2,1,0:T(8,128)(2,1)S(1)} %rows.1), channel_id=1, replica_groups=mesh['line'=16,'view'=2] {'line','view'}, dimensions={0} | all-to-all | bytes 131072 | tf_op jit(solution)/shard_map/all_to_all | solution.py:275
  17.8 0.0 copy-done.2
  17.8 0.0 copy-done.3
  17.8 0.0 copy-done.4
  17.8 0.0 copy-done.5
  17.8 1.7 %columns.1 = bf16[32,5,8,128]{3,2,1,0:T(8,128)(2,1)S(1)} custom-call(bf16[32,8,128]{2,1,0:T(8,128)(2,1)S(1)} %all_to_all.10.x_ref, bf16[2,64,128]{2,1,0:T(8,128)(2,1)S(1)} %copy-done.2, bf16[2,64,128]{2,1,0:T(8,128)(2,1)S(1)} %copy-done.3, bf16[2,64,128]{2,1,0:T(8,128)(2,1)S(1)} %copy-done.4, bf16[2,64,128]{2,1,0:T(8,128)(2,1)S(1)} %bitcast.3), custom_call_target="tpu_custom_call" | custom-call | tf_op jit(solution)/shard_map/columns/pallas_call | solution.py:277
  19.5 0.0 copy-start
  19.5 0.0 copy-start.1
  19.5 13.5 %all_to_all.11.x_ref = bf16[32,5,8,128]{3,2,1,0:T(8,128)(2,1)S(1)} all-to-all(bf16[32,5,8,128]{3,2,1,0:T(8,128)(2,1)S(1)} %columns.1), channel_id=1, replica_groups=mesh['line'=16,'view'=2] {'line','view'}, dimensions={0} | all-to-all | bytes 655360 | tf_op jit(solution)/shard_map/all_to_all | solution.py:284
  33.1 0.0 copy-done
  33.1 0.0 copy-done.1
  33.1 1.3 %convs.1 = bf16[8,4,1024]{2,1,0:T(4,128)(2,1)} custom-call(bf16[32,5,8,128]{3,2,1,0:T(8,128)(2,1)S(1)} %all_to_all.11.x_ref, bf16[3,3,64,64]{3,2,1,0:T(8,128)(2,1)S(1)} %copy-done, bf16[3,3,64,64]{3,2,1,0:T(8,128)(2,1)S(1)} %copy-done.1), custom_call_target="tpu_custom_call" | custom-call | tf_op jit(solution)/shard_map/convs/pallas_call | solution.py:285
Async XLA Ops:
  3.0 14.8 %copy-start.2 = (bf16[2,64,128]{2,1,0:T(8,128)(2,1)S(1)}, bf16[2,64,128]{2,1,0:T(8,128)(2,1)}, u32[]{:S(2)}) copy-start(bf16[2,64,128]{2,1,0:T(8,128)(2,1)} %wq_ref.1) | copy-start | bytes 98308
  3.0 14.8 %copy-start.3 = (bf16[2,64,128]{2,1,0:T(8,128)(2,1)S(1)}, bf16[2,64,128]{2,1,0:T(8,128)(2,1)}, u32[]{:S(2)}) copy-start(bf16[2,64,128]{2,1,0:T(8,128)(2,1)} %wk_ref.1) | copy-start | bytes 98308
  3.0 14.8 %copy-start.4 = (bf16[2,64,128]{2,1,0:T(8,128)(2,1)S(1)}, bf16[2,64,128]{2,1,0:T(8,128)(2,1)}, u32[]{:S(2)}) copy-start(bf16[2,64,128]{2,1,0:T(8,128)(2,1)} %wv_ref.1) | copy-start | bytes 98308
  3.0 14.8 %copy-start.5 = (bf16[2,128,64]{1,2,0:T(8,128)(2,1)S(1)}, bf16[2,128,64]{1,2,0:T(8,128)(2,1)}, u32[]{:S(2)}) copy-start(bf16[2,128,64]{1,2,0:T(8,128)(2,1)} %param.11) | copy-start | bytes 98308
  19.5 13.6 %copy-start = (bf16[3,3,64,64]{3,2,1,0:T(8,128)(2,1)S(1)}, bf16[3,3,64,64]{3,2,1,0:T(8,128)(2,1)}, u32[]{:S(2)}) copy-start(bf16[3,3,64,64]{3,2,1,0:T(8,128)(2,1)} %first_ref.1) | copy-start | bytes 221188
  19.5 13.6 %copy-start.1 = (bf16[3,3,64,64]{3,2,1,0:T(8,128)(2,1)S(1)}, bf16[3,3,64,64]{3,2,1,0:T(8,128)(2,1)}, u32[]{:S(2)}) copy-start(bf16[3,3,64,64]{3,2,1,0:T(8,128)(2,1)} %second_ref.1) | copy-start | bytes 221188

commit v3 on v2

v3 whole, which is shorter than its diff:
```python
import functools
import math

import jax
import jax.numpy as jnp
from jax import lax
from jax.experimental import pallas as pl
from jax.experimental.pallas import tpu as pltpu
from jax.sharding import PartitionSpec as P

AXES = ("line", "view")
QUERY_BLOCK = 256
F32 = jnp.float32
BF16 = jnp.bfloat16
SUBLANES = 8
VMEM_BYTES = 16 * 1024 * 1024


def block_ones(lanes, channels):
    rows = lax.broadcasted_iota(jnp.int32, (lanes, lanes), 0) // channels
    cols = lax.broadcasted_iota(jnp.int32, (lanes, lanes), 1) // channels
    return jnp.where(rows == cols, 1.0 / channels, 0.0).astype(F32)


def packed_norm(tokens, channels):
    ones = block_ones(tokens.shape[-1], channels)
    mean = jnp.dot(tokens.astype(BF16), ones.astype(BF16), preferred_element_type=F32)
    centre = tokens - mean
    spread = jnp.dot(
        centre * centre, ones, precision=lax.Precision.HIGHEST, preferred_element_type=F32
    )
    return (centre * lax.rsqrt(spread + 1e-05)).astype(BF16)


def project_halves(normed, query_matrix, key_matrix, value_matrix):
    joined = jnp.concatenate([query_matrix, key_matrix, value_matrix], axis=1)
    nothing = jnp.zeros_like(joined)
    halves = []
    for parts in ([joined, nothing], [nothing, joined]):
        matrix = jnp.concatenate(parts, axis=0)
        halves.append(jnp.dot(normed, matrix, preferred_element_type=F32).astype(BF16))
    return halves


def attend_rows(queries, keys, values, scaling):
    scores = (
        lax.dot_general(queries, keys, (((1,), (1,)), ((), ())), preferred_element_type=F32)
        * scaling
    )
    exponent = jnp.exp(scores - jnp.max(scores, axis=-1, keepdims=True))
    weights = (exponent / jnp.sum(exponent, axis=-1, keepdims=True)).astype(BF16)
    return jnp.dot(weights, values, preferred_element_type=F32).astype(BF16)


def attend_line(queries, keys, values, scaling, scratch):
    tokens, width = queries.shape
    if tokens <= QUERY_BLOCK:
        return attend_rows(queries, keys, values, scaling)
    scratch[0] = queries
    scratch[1] = keys
    scratch[2] = values

    def block(index, carry):
        rows = pl.ds(pl.multiple_of(index * QUERY_BLOCK, QUERY_BLOCK), QUERY_BLOCK)
        scratch[3, rows, :] = attend_rows(scratch[0, rows, :], scratch[1], scratch[2], scaling)
        return carry

    lax.fori_loop(0, tokens // QUERY_BLOCK, block, 0)
    return scratch[3]


def out_halves(flipped):
    nothing = jnp.zeros_like(flipped)
    return jnp.concatenate(
        [
            jnp.concatenate([flipped, nothing], axis=1),
            jnp.concatenate([nothing, flipped], axis=1),
        ],
        axis=0,
    )


def project_out(mixed, out_matrix):
    return lax.dot_general(
        mixed, out_matrix, (((1,), (1,)), ((), ())), preferred_element_type=F32
    )


def rows_kernel(
    x_hbm,
    wq_hbm,
    wk_hbm,
    wv_hbm,
    wo_hbm,
    o_ref,
    held,
    spread,
    leaving,
    lines,
    x_ref,
    wq_ref,
    wk_ref,
    wv_ref,
    wo_ref,
    arrivals,
):
    pulls = [
        (x_hbm, x_ref),
        (wq_hbm, wq_ref),
        (wk_hbm, wk_ref),
        (wv_hbm, wv_ref),
        (wo_hbm, wo_ref),
    ]
    copies = [
        pltpu.make_async_copy(source.at[0], target, arrivals.at[index])
        for index, (source, target) in enumerate(pulls)
    ]
    for copy in copies:
        copy.start()
    all_u, local_v, packed = x_ref.shape
    channels, width = wq_ref.shape
    lanes = 2 * channels
    pairs = packed // lanes
    per_line = pairs * all_u
    owners, chunk = o_ref.shape[:2]
    window = chunk // local_v
    own = window - 2
    scaling = 1.0 / math.sqrt(width)
    copies[0].wait()
    for u in range(all_u):
        rows = x_ref[u].astype(F32)
        for pair in range(pairs):
            held[pl.ds((u * pairs + pair) * local_v, local_v), :] = rows[
                :, pair * lanes : (pair + 1) * lanes
            ]
    tokens = jnp.concatenate(
        [held[pl.ds(v, per_line, stride=local_v), :] for v in range(local_v)], axis=0
    )
    normed = packed_norm(tokens, channels)
    for copy in copies[1:]:
        copy.wait()
    low, high = project_halves(normed, wq_ref[...], wk_ref[...], wv_ref[...])
    out_matrix = out_halves(wo_ref[...])
    place = lax.broadcasted_iota(jnp.int32, (owners, lanes), 0) % (pairs // own)
    for v in range(local_v):
        span = slice(v * per_line, (v + 1) * per_line)
        both = jnp.concatenate([low[span], high[span]], axis=0)
        mixed = attend_line(
            both[:, :width], both[:, width : 2 * width], both[:, 2 * width :], scaling, lines
        )
        mixed = jnp.concatenate([mixed[:per_line], mixed[per_line:]], axis=1)
        spread[v, pl.ds(SUBLANES, per_line), :] = tokens[span] + project_out(mixed, out_matrix)
        for step in range(window):
            part = spread[v, pl.ds(SUBLANES - 1 + step, owners, stride=own), :]
            if step == 0:
                part = jnp.where(place == 0, 0.0, part)
            if step == window - 1:
                part = jnp.where(place == pairs // own - 1, 0.0, part)
            leaving[pl.ds(v * window + step, owners, stride=chunk), :] = part
    o_ref[...] = leaving[...].astype(BF16).reshape(o_ref.shape)


def pair_weights(kernel):
    nothing = jnp.zeros_like(kernel[0, 0])
    parts = []
    for row in range(3):
        left, middle, right = kernel[row, 0], kernel[row, 1], kernel[row, 2]
        parts += [
            jnp.concatenate([middle, left], axis=1),
            jnp.concatenate([right, middle], axis=1),
            jnp.concatenate([nothing, right], axis=1),
            jnp.concatenate([left, nothing], axis=1),
        ]
    return jnp.concatenate(parts, axis=0)


def neighbourhood(before, image, after, row):
    lane = lax.broadcasted_iota(jnp.int32, image.shape, 1)
    wide = jnp.concatenate(
        [image, jnp.where(lane < image.shape[1] // 2, after, before)], axis=1
    )
    blank = jnp.zeros((row, wide.shape[1]), wide.dtype)
    above = jnp.concatenate([blank, wide[:-row]], axis=0)
    below = jnp.concatenate([wide[row:], blank], axis=0)
    return jnp.concatenate([above, wide, below], axis=1).astype(BF16)


def columns_kernel(
    x_ref,
    wq_ref,
    wk_ref,
    wv_ref,
    wo_ref,
    first_ref,
    second_ref,
    o_ref,
    held,
    leaving,
    lines,
    *,
    local_v,
    views,
    places,
):
    sources, chunk, lanes = x_ref.shape
    channels, width = wq_ref.shape[1:]
    window = chunk // local_v
    own = window - 2
    per_line = sources * local_v
    row = views * local_v
    scaling = 1.0 / math.sqrt(width)
    held[...] = x_ref[...].astype(F32).reshape(held.shape)
    tokens = jnp.concatenate(
        [held[pl.ds(step, per_line, stride=window), :] for step in range(window)], axis=0
    )
    normed = packed_norm(tokens, channels)
    halves = project_halves(normed, wq_ref[1], wk_ref[1], wv_ref[1])
    out_matrix = out_halves(wo_ref[1])
    images = []
    for step in range(window):
        span = slice(step * per_line, (step + 1) * per_line)
        mixed = [
            attend_line(
                half[span, :width],
                half[span, width : 2 * width],
                half[span, 2 * width :],
                scaling,
                lines,
            )
            for half in halves
        ]
        summed = tokens[span] + project_out(jnp.concatenate(mixed, axis=1), out_matrix)
        images.append(summed.astype(BF16).astype(F32))

    blank = jnp.zeros_like(images[0])
    edged = [blank, *images, blank]
    summed = jnp.dot(
        jnp.concatenate(
            [neighbourhood(*edged[step : step + 3], row) for step in range(window)], axis=0
        ),
        pair_weights(first_ref[...]),
        preferred_element_type=F32,
    )
    active = jnp.where(summed >= 0, summed, 0.1 * summed).astype(BF16).astype(F32)
    place = (lax.axis_index("line") * views + lax.axis_index("view")) % places
    hidden = [active[step * per_line : (step + 1) * per_line] for step in range(window)]
    hidden[0] = jnp.where(place > 0, hidden[0], 0.0)
    hidden[-1] = jnp.where(place < places - 1, hidden[-1], 0.0)
    summed = jnp.dot(
        jnp.concatenate(
            [neighbourhood(*hidden[step : step + 3], row) for step in range(own)], axis=0
        ),
        pair_weights(second_ref[...]),
        preferred_element_type=F32,
    )
    for step in range(own):
        leaving[pl.ds(step, per_line, stride=own), :] = (
            images[step + 1] + summed[step * per_line : (step + 1) * per_line]
        )
    o_ref[...] = leaving[...].astype(BF16).reshape(o_ref.shape)


def place_kernel(x_ref, o_ref, held):
    sources, chunk, lanes = x_ref.shape
    all_u, local_v, packed = o_ref.shape
    own = chunk // local_v
    places = sources // all_u
    held[...] = x_ref[...].astype(F32).reshape(held.shape)
    for source in range(sources):
        u, place = source // places, source % places
        for step in range(own):
            start = (place * own + step) * lanes
            o_ref[u, :, start : start + lanes] = held[
                pl.ds(source * chunk + step, local_v, stride=own), :
            ].astype(BF16)


def local(light_field, query_weight, key_weight, value_weight, out_weight, conv_first, conv_second):
    span_rows, all_u, local_v, packed = light_field.shape
    channels, width = query_weight.shape[1:]
    lanes = 2 * channels
    lines, views = lax.axis_size("line"), lax.axis_size("view")
    devices = lines * views
    pairs = packed // lanes
    packed_lines = pairs * all_u
    own = packed_lines // devices
    if span_rows != 1 or packed_lines % devices or pairs % own:
        raise ValueError("unsupported split")
    window = own + 2
    places = pairs // own

    weights = (query_weight, key_weight, value_weight, out_weight.transpose(0, 2, 1))
    params = pltpu.CompilerParams(vmem_limit_bytes=VMEM_BYTES)

    def scratch(tokens):
        kept = tokens if tokens > QUERY_BLOCK else 16
        return pltpu.VMEM((4, kept, width), BF16)

    leaving = pl.pallas_call(
        rows_kernel,
        out_shape=jax.ShapeDtypeStruct((devices, local_v * window, lanes), BF16),
        in_specs=[pl.BlockSpec(memory_space=pltpu.HBM)] * 5,
        scratch_shapes=[
            pltpu.VMEM((packed_lines * local_v, lanes), F32),
            pltpu.VMEM((local_v, packed_lines + 2 * SUBLANES, lanes), F32),
            pltpu.VMEM((devices * local_v * window, lanes), F32),
            scratch(2 * packed_lines),
            pltpu.VMEM((all_u, local_v, packed), BF16),
            *[pltpu.VMEM((channels, width), BF16)] * 4,
            pltpu.SemaphoreType.DMA((5,)),
        ],
        compiler_params=params,
        name="rows",
    )(*(pltpu.with_memory_space_constraint(a, pltpu.HBM) for a in (light_field, *weights)))
    arrived = lax.all_to_all(leaving, AXES, split_axis=0, concat_axis=0, tiled=True)
    finished = pl.pallas_call(
        functools.partial(columns_kernel, local_v=local_v, views=views, places=places),
        out_shape=jax.ShapeDtypeStruct((devices, local_v * own, lanes), BF16),
        scratch_shapes=[
            pltpu.VMEM((devices * local_v * window, lanes), F32),
            pltpu.VMEM((devices * local_v * own, lanes), F32),
            scratch(devices * local_v),
        ],
        compiler_params=params,
        name="columns",
    )(arrived, *weights, conv_first, conv_second)
    returned = lax.all_to_all(finished, AXES, split_axis=0, concat_axis=0, tiled=True)
    result = pl.pallas_call(
        place_kernel,
        out_shape=jax.ShapeDtypeStruct((all_u, local_v, packed), BF16),
        scratch_shapes=[pltpu.VMEM((devices * local_v * own, lanes), F32)],
        compiler_params=params,
        name="place",
    )(returned)
    return result[None]


def solution(mesh):
    placed = (P("line", None, "view", None), P(), P(), P(), P(), P(), P())
    return jax.shard_map(
        local, mesh=mesh, in_specs=placed, out_specs=P("line", None, "view", None), check_vma=False
    )
```

time: 34.7 us -> 32.7 us (0.942)
  blocking collectives: 28.3 us -> 25 us
  Pallas kernels: 6.01 us -> 7.36 us
    all_to_all x1, blocking collectives: 13.5 us -> 9.3 us  [local(): lax.all_to_all(finished, AXES, split_axis=0, concat_axis=0, tiled=True)]
    pallas_call x1, Pallas kernels: 1.73 us -> 3.67 us  [local(): pl.pallas_call(functools.partial(columns_kernel, local_v=local_v, views=v...]
    all_to_all x1, blocking collectives: 14.7 us -> 15.7 us  [local(): lax.all_to_all(leaving, AXES, split_axis=0, concat_axis=0, tiled=True)]
    pallas_call x2, Pallas kernels: 4.28 us -> 3.69 us  [the longest x1 3.02 us: local(): pl.pallas_call(rows_kernel, out_shape=jax.ShapeDtypeStruct((devices, loca...]
where the time goes in v3:
time: 32.7 us; the launch traced here: 32.5 us
  blocking collectives  25 us (76%)
  Pallas kernels  7.36 us (23%)
    all_to_all x1, blocking collectives, local(): lax.all_to_all(leaving, AXES, split_axis=0, concat_axis=0, tiled=True)  15.7 us
    all_to_all x1, blocking collectives, local(): lax.all_to_all(finished, AXES, split_axis=0, concat_axis=0, tiled=True)  9.3 us
    pallas_call x1, Pallas kernels, local(): pl.pallas_call(functools.partial(columns_kernel, local_v=local_v, views=v...  3.67 us
    pallas_call x1, Pallas kernels, local(): pl.pallas_call(rows_kernel, out_shape=jax.ShapeDtypeStruct((devices, loca...  3.02 us
    pallas_call x1, Pallas kernels, local(): pl.pallas_call(place_kernel, out_shape=jax.ShapeDtypeStruct((all_u, local...  0.67 us

profile of v3, /device:TPU:0, one launch (start us, length us, event | category | flops | bytes accessed | tf_op | source)
XLA Modules:
  0.0 32.5 jit_solution(7586539935560320861)
XLA Ops:
  0.0 0.0 copy-start.1
  0.0 0.0 copy-start.5
  0.0 3.0 %rows.1 = bf16[32,16,128]{2,1,0:T(8,128)(2,1)S(1)} custom-call(bf16[1,8,4,1024]{3,2,1,0:T(4,128)(2,1)} %x_hbm.1, bf16[2,64,128]{2,1,0:T(8,128)(2,1)} %wq_ref.1, bf16[2,64,128]{2,1,0:T(8,128)(2,1)} %wk_ref.1, bf16[2,64,128]{2,1,0:T(8,128)(2,1)} %wv_ref.1, bf16[2,64,128]{2,1,0:T(8,128)(2,1)} %bitcast.2), custom_call_target="tpu_custom_call" | custom-call | tf_op jit(solution)/shard_map/rows/pallas_call | solution.py:299
  3.0 0.0 copy-start
  3.0 0.0 copy-start.2
  3.1 0.0 copy-start.3
  3.1 0.0 copy-start.4
  3.1 15.7 %all_to_all.10.x_ref = bf16[32,16,128]{2,1,0:T(8,128)(2,1)S(1)} all-to-all(bf16[32,16,128]{2,1,0:T(8,128)(2,1)S(1)} %rows.1), channel_id=1, replica_groups=mesh['line'=16,'view'=2] {'line','view'}, dimensions={0} | all-to-all | bytes 262144 | tf_op jit(solution)/shard_map/all_to_all | solution.py:315
  18.8 0.0 copy-done.1
  18.8 0.0 copy-done.5
  18.8 0.0 copy-done
  18.8 0.0 copy-done.2
  18.8 0.0 copy-done.3
  18.8 0.0 copy-done.4
  18.9 3.7 %columns.1 = bf16[32,8,128]{2,1,0:T(8,128)(2,1)S(1)} custom-call(bf16[32,16,128]{2,1,0:T(8,128)(2,1)S(1)} %all_to_all.10.x_ref, bf16[2,64,128]{2,1,0:T(8,128)(2,1)S(1)} %copy-done.2, bf16[2,64,128]{2,1,0:T(8,128)(2,1)S(1)} %copy-done.3, bf16[2,64,128]{2,1,0:T(8,128)(2,1)S(1)} %copy-done.4, bf16[2,64,128]{2,1,0:T(8,128)(2,1)S(1)} %bitcast.3, ...), custom_call_target="tpu_custom_call" | custom-call | tf_op jit(solution)/shard_map/columns/pallas_call | solution.py:316
  22.5 9.3 %all_to_all.11.x_ref = bf16[32,8,128]{2,1,0:T(8,128)(2,1)S(1)} all-to-all(bf16[32,8,128]{2,1,0:T(8,128)(2,1)S(1)} %columns.1), channel_id=1, replica_groups=mesh['line'=16,'view'=2] {'line','view'}, dimensions={0} | all-to-all | bytes 131072 | tf_op jit(solution)/shard_map/all_to_all | solution.py:327
  31.8 0.7 %place.1 = bf16[8,4,1024]{2,1,0:T(4,128)(2,1)} custom-call(bf16[32,8,128]{2,1,0:T(8,128)(2,1)S(1)} %all_to_all.11.x_ref), custom_call_target="tpu_custom_call" | custom-call | tf_op jit(solution)/shard_map/place/pallas_call | solution.py:328
Async XLA Ops:
  0.0 18.8 %copy-start.1 = (bf16[3,3,64,64]{3,2,1,0:T(8,128)(2,1)S(1)}, bf16[3,3,64,64]{3,2,1,0:T(8,128)(2,1)}, u32[]{:S(2)}) copy-start(bf16[3,3,64,64]{3,2,1,0:T(8,128)(2,1)} %second_ref.1) | copy-start | bytes 221188
  0.0 18.8 %copy-start.5 = (bf16[2,128,64]{1,2,0:T(8,128)(2,1)S(1)}, bf16[2,128,64]{1,2,0:T(8,128)(2,1)}, u32[]{:S(2)}) copy-start(bf16[2,128,64]{1,2,0:T(8,128)(2,1)} %param.11) | copy-start | bytes 98308
  3.0 15.8 %copy-start = (bf16[3,3,64,64]{3,2,1,0:T(8,128)(2,1)S(1)}, bf16[3,3,64,64]{3,2,1,0:T(8,128)(2,1)}, u32[]{:S(2)}) copy-start(bf16[3,3,64,64]{3,2,1,0:T(8,128)(2,1)} %first_ref.1) | copy-start | bytes 221188
  3.0 15.8 %copy-start.2 = (bf16[2,64,128]{2,1,0:T(8,128)(2,1)S(1)}, bf16[2,64,128]{2,1,0:T(8,128)(2,1)}, u32[]{:S(2)}) copy-start(bf16[2,64,128]{2,1,0:T(8,128)(2,1)} %wq_ref.1) | copy-start | bytes 98308
  3.1 15.8 %copy-start.3 = (bf16[2,64,128]{2,1,0:T(8,128)(2,1)S(1)}, bf16[2,64,128]{2,1,0:T(8,128)(2,1)}, u32[]{:S(2)}) copy-start(bf16[2,64,128]{2,1,0:T(8,128)(2,1)} %wk_ref.1) | copy-start | bytes 98308
  3.1 15.8 %copy-start.4 = (bf16[2,64,128]{2,1,0:T(8,128)(2,1)S(1)}, bf16[2,64,128]{2,1,0:T(8,128)(2,1)}, u32[]{:S(2)}) copy-start(bf16[2,64,128]{2,1,0:T(8,128)(2,1)} %wv_ref.1) | copy-start | bytes 98308

commit v4 on v3

v4 whole, which is shorter than its diff:
```python
import functools
import math

import jax
import jax.numpy as jnp
from jax import lax
from jax.experimental import pallas as pl
from jax.experimental.pallas import tpu as pltpu
from jax.sharding import PartitionSpec as P

AXES = ("line", "view")
QUERY_BLOCK = 256
F32 = jnp.float32
BF16 = jnp.bfloat16
SUBLANES = 8
VMEM_BYTES = 16 * 1024 * 1024


def block_ones(lanes, channels):
    rows = lax.broadcasted_iota(jnp.int32, (lanes, lanes), 0) // channels
    cols = lax.broadcasted_iota(jnp.int32, (lanes, lanes), 1) // channels
    return jnp.where(rows == cols, 1.0 / channels, 0.0).astype(F32)


def packed_norm(tokens, channels):
    ones = block_ones(tokens.shape[-1], channels)
    mean = jnp.dot(tokens.astype(BF16), ones.astype(BF16), preferred_element_type=F32)
    centre = tokens - mean
    square = centre * centre
    upper = square.astype(BF16)
    lower = (square - upper.astype(F32)).astype(BF16)
    spread = jnp.dot(
        jnp.concatenate([upper, lower], axis=1),
        jnp.concatenate([ones, ones], axis=0).astype(BF16),
        preferred_element_type=F32,
    )
    return (centre * lax.rsqrt(spread + 1e-05)).astype(BF16)


def folded_values(value_matrix, flipped):
    return lax.dot_general(
        value_matrix, flipped, (((1,), (1,)), ((), ())), preferred_element_type=F32
    ).astype(BF16)


def both_halves(*parts):
    lower, upper = [], []
    for first, second in parts:
        lower.append(jnp.zeros_like(second) if first is None else first)
        upper.append(jnp.zeros_like(first) if second is None else second)
    return jnp.concatenate(
        [jnp.concatenate(lower, axis=1), jnp.concatenate(upper, axis=1)], axis=0
    )


def exponents(queries, keys, scaling):
    scores = lax.dot_general(
        queries, keys, (((1,), (1,)), ((), ())), preferred_element_type=F32
    )
    top = jnp.max(scores, axis=-1, keepdims=True)
    return jnp.exp((scores - top) * scaling).astype(BF16)


def weigh(low, high, values):
    rows, lanes = low.shape[0], values.shape[1] // 2
    summed = jnp.dot(
        jnp.concatenate([low, high], axis=0), values, preferred_element_type=F32
    )
    lane = lax.broadcasted_iota(jnp.int32, (rows, 2 * lanes), 1) % lanes
    chosen = jnp.where(lane < lanes // 2, summed[:rows], summed[rows:])
    return chosen[:, :lanes] / chosen[:, lanes:]


def attend_pair(low, high, keys, values, scaling, pieces, mixed):
    count = low.shape[0]
    values = jnp.concatenate([values, jnp.ones_like(values)], axis=1)
    if count <= QUERY_BLOCK:
        if len(keys) == 1:
            both = exponents(jnp.concatenate([low, high], axis=0), keys[0], scaling)
            return weigh(both[:count], both[count:], values)
        return weigh(
            exponents(low, keys[0], scaling), exponents(high, keys[1], scaling), values
        )
    width = low.shape[1]
    key_count = values.shape[0]
    for index, part in enumerate([low, high]):
        pieces[index, :count] = part
    for index, part in enumerate([keys[0], keys[-1], values[:, :width], values[:, width:]]):
        pieces[2 + index, :key_count] = part

    def block(index, carry):
        rows = pl.ds(pl.multiple_of(index * QUERY_BLOCK, QUERY_BLOCK), QUERY_BLOCK)
        mixed[rows, :] = weigh(
            exponents(pieces[0, rows, :], pieces[2, :key_count], scaling),
            exponents(pieces[1, rows, :], pieces[3, :key_count], scaling),
            jnp.concatenate([pieces[4, :key_count], pieces[5, :key_count]], axis=1),
        )
        return carry

    lax.fori_loop(0, count // QUERY_BLOCK, block, 0)
    return mixed[:count]


def rows_kernel(
    x_hbm,
    wq_hbm,
    wk_hbm,
    wv_hbm,
    wo_hbm,
    o_ref,
    held,
    spread,
    leaving,
    lines,
    mixed,
    x_ref,
    wq_ref,
    wk_ref,
    wv_ref,
    wo_ref,
    arrivals,
):
    pulls = [
        (x_hbm, x_ref),
        (wq_hbm, wq_ref),
        (wk_hbm, wk_ref),
        (wv_hbm, wv_ref),
        (wo_hbm, wo_ref),
    ]
    copies = [
        pltpu.make_async_copy(source.at[0], target, arrivals.at[index])
        for index, (source, target) in enumerate(pulls)
    ]
    for copy in copies:
        copy.start()
    all_u, local_v, packed = x_ref.shape
    channels, width = wq_ref.shape
    lanes = 2 * channels
    pairs = packed // lanes
    per_line = pairs * all_u
    owners, chunk = o_ref.shape[:2]
    window = chunk // local_v
    own = window - 2
    scaling = 1.0 / math.sqrt(width)
    copies[0].wait()
    for u in range(all_u):
        rows = x_ref[u].astype(F32)
        for pair in range(pairs):
            held[pl.ds((u * pairs + pair) * local_v, local_v), :] = rows[
                :, pair * lanes : (pair + 1) * lanes
            ]
    tokens = jnp.concatenate(
        [held[pl.ds(v, per_line, stride=local_v), :] for v in range(local_v)], axis=0
    )
    normed = packed_norm(tokens, channels)
    for copy in copies[1:]:
        copy.wait()
    query_matrix, key_matrix = wq_ref[...], wk_ref[...]
    folded = folded_values(wv_ref[...], wo_ref[...])
    projected = jnp.dot(
        normed,
        both_halves(
            (query_matrix, None),
            (key_matrix, None),
            (folded, None),
            (folded, None),
            (None, query_matrix),
            (None, key_matrix),
            (None, folded),
            (None, folded),
        ),
        preferred_element_type=F32,
    ).astype(BF16)
    part = 2 * width + lanes
    place = lax.broadcasted_iota(jnp.int32, (owners, lanes), 0) % (pairs // own)
    for v in range(local_v):
        span = slice(v * per_line, (v + 1) * per_line)
        both = jnp.concatenate([projected[span, :part], projected[span, part:]], axis=0)
        summed = tokens[span] + attend_pair(
            both[:per_line, :width],
            both[per_line:, :width],
            [both[:, width : 2 * width]],
            both[:, 2 * width :],
            scaling,
            lines,
            mixed,
        )
        spread[v, pl.ds(SUBLANES, per_line), :] = summed
        for step in range(window):
            piece = spread[v, pl.ds(SUBLANES - 1 + step, owners, stride=own), :]
            if step == 0:
                piece = jnp.where(place == 0, 0.0, piece)
            if step == window - 1:
                piece = jnp.where(place == pairs // own - 1, 0.0, piece)
            leaving[pl.ds(v * window + step, owners, stride=chunk), :] = piece
    o_ref[...] = leaving[...].astype(BF16).reshape(o_ref.shape)


def pair_weights(kernel):
    nothing = jnp.zeros_like(kernel[0, 0])
    parts = [[], [], [], []]
    for row in range(3):
        left, middle, right = kernel[row, 0], kernel[row, 1], kernel[row, 2]
        parts[0] += [middle, left]
        parts[1] += [right, middle]
        parts[2] += [nothing, right]
        parts[3] += [left, nothing]
    return jnp.concatenate([jnp.concatenate(part, axis=1) for part in parts], axis=0)


def correlate(images, weights, row):
    count, lanes = images[0].shape
    lane = lax.broadcasted_iota(jnp.int32, (count, lanes), 1)
    wide = [
        jnp.concatenate([image, jnp.where(lane < lanes // 2, after, before)], axis=1)
        for before, image, after in zip(images, images[1:], images[2:])
    ]
    terms = jnp.dot(jnp.concatenate(wide, axis=0), weights, preferred_element_type=F32)
    blank = jnp.zeros((row, lanes), F32)
    results = []
    for step in range(len(wide)):
        span = terms[step * count : (step + 1) * count]
        above = jnp.concatenate([blank, span[:-row, :lanes]], axis=0)
        below = jnp.concatenate([span[row:, 2 * lanes :], blank], axis=0)
        results.append(above + span[:, lanes : 2 * lanes] + below)
    return results


def columns_kernel(
    x_ref,
    wq_ref,
    wk_ref,
    wv_ref,
    wo_ref,
    first_ref,
    second_ref,
    o_ref,
    held,
    leaving,
    lines,
    mixed,
    *,
    local_v,
    views,
    places,
):
    sources, chunk, lanes = x_ref.shape
    channels, width = wq_ref.shape[1:]
    window = chunk // local_v
    own = window - 2
    per_line = sources * local_v
    row = views * local_v
    scaling = 1.0 / math.sqrt(width)
    held[...] = x_ref[...].astype(F32).reshape(held.shape)
    tokens = jnp.concatenate(
        [held[pl.ds(step, per_line, stride=window), :] for step in range(window)], axis=0
    )
    normed = packed_norm(tokens, channels)
    query_matrix, key_matrix = wq_ref[1], wk_ref[1]
    folded = folded_values(wv_ref[1], wo_ref[1])
    projected = jnp.dot(
        normed,
        both_halves(
            (query_matrix, None),
            (key_matrix, None),
            (None, query_matrix),
            (None, key_matrix),
            (folded, None),
            (None, folded),
        ),
        preferred_element_type=F32,
    ).astype(BF16)
    images = []
    for step in range(window):
        span = slice(step * per_line, (step + 1) * per_line)
        queries_keys = [projected[span, i * width : (i + 1) * width] for i in range(4)]
        summed = tokens[span] + attend_pair(
            queries_keys[0],
            queries_keys[2],
            queries_keys[1::2],
            projected[span, 4 * width :],
            scaling,
            lines,
            mixed,
        )
        images.append(summed.astype(BF16))

    blank = jnp.zeros_like(images[0])
    hidden = [
        jnp.where(value >= 0, value, 0.1 * value)
        for value in correlate([blank, *images, blank], pair_weights(first_ref[...]), row)
    ]
    place = (lax.axis_index("line") * views + lax.axis_index("view")) % places
    hidden[0] = jnp.where(place > 0, hidden[0], 0.0)
    hidden[-1] = jnp.where(place < places - 1, hidden[-1], 0.0)
    hidden = [value.astype(BF16) for value in hidden]
    for step, value in enumerate(correlate(hidden, pair_weights(second_ref[...]), row)):
        leaving[pl.ds(step, per_line, stride=own), :] = images[step + 1].astype(F32) + value
    o_ref[...] = leaving[...].astype(BF16).reshape(o_ref.shape)


def place_kernel(x_ref, o_ref, held):
    sources, chunk, lanes = x_ref.shape
    all_u, local_v, packed = o_ref.shape
    own = chunk // local_v
    places = sources // all_u
    held[...] = x_ref[...].astype(F32).reshape(held.shape)
    for source in range(sources):
        u, place = source // places, source % places
        for step in range(own):
            start = (place * own + step) * lanes
            o_ref[u, :, start : start + lanes] = held[
                pl.ds(source * chunk + step, local_v, stride=own), :
            ].astype(BF16)


def local(light_field, query_weight, key_weight, value_weight, out_weight, conv_first, conv_second):
    span_rows, all_u, local_v, packed = light_field.shape
    channels, width = query_weight.shape[1:]
    lanes = 2 * channels
    lines, views = lax.axis_size("line"), lax.axis_size("view")
    devices = lines * views
    pairs = packed // lanes
    packed_lines = pairs * all_u
    own = packed_lines // devices
    if span_rows != 1 or packed_lines % devices or pairs % own:
        raise ValueError("unsupported split")
    window = own + 2
    places = pairs // own

    weights = (query_weight, key_weight, value_weight, out_weight.transpose(0, 2, 1))
    params = pltpu.CompilerParams(vmem_limit_bytes=VMEM_BYTES)

    def scratch(tokens):
        kept = tokens if tokens > QUERY_BLOCK else 16
        return [pltpu.VMEM((6, kept, width), BF16), pltpu.VMEM((kept, lanes), F32)]

    leaving = pl.pallas_call(
        rows_kernel,
        out_shape=jax.ShapeDtypeStruct((devices, local_v * window, lanes), BF16),
        in_specs=[pl.BlockSpec(memory_space=pltpu.HBM)] * 5,
        scratch_shapes=[
            pltpu.VMEM((packed_lines * local_v, lanes), F32),
            pltpu.VMEM((local_v, packed_lines + 2 * SUBLANES, lanes), F32),
            pltpu.VMEM((devices * local_v * window, lanes), F32),
            *scratch(2 * packed_lines),
            pltpu.VMEM((all_u, local_v, packed), BF16),
            *[pltpu.VMEM((channels, width), BF16)] * 4,
            pltpu.SemaphoreType.DMA((5,)),
        ],
        compiler_params=params,
        name="rows",
    )(*(pltpu.with_memory_space_constraint(a, pltpu.HBM) for a in (light_field, *weights)))
    arrived = lax.all_to_all(leaving, AXES, split_axis=0, concat_axis=0, tiled=True)
    finished = pl.pallas_call(
        functools.partial(columns_kernel, local_v=local_v, views=views, places=places),
        out_shape=jax.ShapeDtypeStruct((devices, local_v * own, lanes), BF16),
        scratch_shapes=[
            pltpu.VMEM((devices * local_v * window, lanes), F32),
            pltpu.VMEM((devices * local_v * own, lanes), F32),
            *scratch(devices * local_v),
        ],
        compiler_params=params,
        name="columns",
    )(arrived, *weights, conv_first, conv_second)
    returned = lax.all_to_all(finished, AXES, split_axis=0, concat_axis=0, tiled=True)
    result = pl.pallas_call(
        place_kernel,
        out_shape=jax.ShapeDtypeStruct((all_u, local_v, packed), BF16),
        scratch_shapes=[pltpu.VMEM((devices * local_v * own, lanes), F32)],
        compiler_params=params,
        name="place",
    )(returned)
    return result[None]


def solution(mesh):
    placed = (P("line", None, "view", None), P(), P(), P(), P(), P(), P())
    return jax.shard_map(
        local, mesh=mesh, in_specs=placed, out_specs=P("line", None, "view", None), check_vma=False
    )
```

time: 32.7 us -> 29.5 us (0.902)
  Pallas kernels: 7.36 us -> 4.2 us
    pallas_call x1, Pallas kernels: 3.67 us -> 1.4 us  [local(): pl.pallas_call(functools.partial(columns_kernel, local_v=local_v, views=v...]
    pallas_call x1, Pallas kernels: 3.02 us -> 2.14 us  [local(): pl.pallas_call(rows_kernel, out_shape=jax.ShapeDtypeStruct((devices, loca...]
where the time goes in v4:
time: 29.5 us; the launch traced here: 29.3 us
  blocking collectives  25 us (85%)
  Pallas kernels  4.2 us (14%)
    all_to_all x1, blocking collectives, local(): lax.all_to_all(leaving, AXES, split_axis=0, concat_axis=0, tiled=True)  15.7 us
    all_to_all x1, blocking collectives, local(): lax.all_to_all(finished, AXES, split_axis=0, concat_axis=0, tiled=True)  9.3 us
    pallas_call x1, Pallas kernels, local(): pl.pallas_call(rows_kernel, out_shape=jax.ShapeDtypeStruct((devices, loca...  2.14 us
    pallas_call x1, Pallas kernels, local(): pl.pallas_call(functools.partial(columns_kernel, local_v=local_v, views=v...  1.4 us
    pallas_call x1, Pallas kernels, local(): pl.pallas_call(place_kernel, out_shape=jax.ShapeDtypeStruct((all_u, local...  0.67 us

profile of v4, /device:TPU:0, one launch (start us, length us, event | category | flops | bytes accessed | tf_op | source)
XLA Modules:
  0.0 29.3 jit_solution(3708909096668653223)
XLA Ops:
  0.0 0.0 copy-start.1
  0.0 0.0 copy-start.5
  0.0 2.1 %rows.1 = bf16[32,16,128]{2,1,0:T(8,128)(2,1)S(1)} custom-call(bf16[1,8,4,1024]{3,2,1,0:T(4,128)(2,1)} %x_hbm.1, bf16[2,64,128]{2,1,0:T(8,128)(2,1)} %wq_ref.1, bf16[2,64,128]{2,1,0:T(8,128)(2,1)} %wk_ref.1, bf16[2,64,128]{2,1,0:T(8,128)(2,1)} %wv_ref.1, bf16[2,64,128]{2,1,0:T(8,128)(2,1)} %bitcast.2), custom_call_target="tpu_custom_call" | custom-call | tf_op jit(solution)/shard_map/rows/pallas_call | solution.py:338
  2.1 0.0 copy-start
  2.2 0.0 copy-start.2
  2.2 0.0 copy-start.3
  2.2 0.0 copy-start.4
  2.2 15.7 %all_to_all.10.x_ref = bf16[32,16,128]{2,1,0:T(8,128)(2,1)S(1)} all-to-all(bf16[32,16,128]{2,1,0:T(8,128)(2,1)S(1)} %rows.1), channel_id=1, replica_groups=mesh['line'=16,'view'=2] {'line','view'}, dimensions={0} | all-to-all | bytes 262144 | tf_op jit(solution)/shard_map/all_to_all | solution.py:354
  17.9 0.0 copy-done.1
  17.9 0.0 copy-done.5
  17.9 0.0 copy-done
  17.9 0.0 copy-done.2
  17.9 0.0 copy-done.3
  18.0 0.0 copy-done.4
  18.0 1.4 %columns.1 = bf16[32,8,128]{2,1,0:T(8,128)(2,1)S(1)} custom-call(bf16[32,16,128]{2,1,0:T(8,128)(2,1)S(1)} %all_to_all.10.x_ref, bf16[2,64,128]{2,1,0:T(8,128)(2,1)S(1)} %copy-done.2, bf16[2,64,128]{2,1,0:T(8,128)(2,1)S(1)} %copy-done.3, bf16[2,64,128]{2,1,0:T(8,128)(2,1)S(1)} %copy-done.4, bf16[2,64,128]{2,1,0:T(8,128)(2,1)S(1)} %bitcast.3, ...), custom_call_target="tpu_custom_call" | custom-call | tf_op jit(solution)/shard_map/columns/pallas_call | solution.py:355
  19.4 9.3 %all_to_all.11.x_ref = bf16[32,8,128]{2,1,0:T(8,128)(2,1)S(1)} all-to-all(bf16[32,8,128]{2,1,0:T(8,128)(2,1)S(1)} %columns.1), channel_id=1, replica_groups=mesh['line'=16,'view'=2] {'line','view'}, dimensions={0} | all-to-all | bytes 131072 | tf_op jit(solution)/shard_map/all_to_all | solution.py:366
  28.7 0.7 %place.1 = bf16[8,4,1024]{2,1,0:T(4,128)(2,1)} custom-call(bf16[32,8,128]{2,1,0:T(8,128)(2,1)S(1)} %all_to_all.11.x_ref), custom_call_target="tpu_custom_call" | custom-call | tf_op jit(solution)/shard_map/place/pallas_call | solution.py:367
Async XLA Ops:
  0.0 17.9 %copy-start.1 = (bf16[3,3,64,64]{3,2,1,0:T(8,128)(2,1)S(1)}, bf16[3,3,64,64]{3,2,1,0:T(8,128)(2,1)}, u32[]{:S(2)}) copy-start(bf16[3,3,64,64]{3,2,1,0:T(8,128)(2,1)} %second_ref.1) | copy-start | bytes 221188
  0.0 17.9 %copy-start.5 = (bf16[2,128,64]{1,2,0:T(8,128)(2,1)S(1)}, bf16[2,128,64]{1,2,0:T(8,128)(2,1)}, u32[]{:S(2)}) copy-start(bf16[2,128,64]{1,2,0:T(8,128)(2,1)} %param.11) | copy-start | bytes 98308
  2.1 15.8 %copy-start = (bf16[3,3,64,64]{3,2,1,0:T(8,128)(2,1)S(1)}, bf16[3,3,64,64]{3,2,1,0:T(8,128)(2,1)}, u32[]{:S(2)}) copy-start(bf16[3,3,64,64]{3,2,1,0:T(8,128)(2,1)} %first_ref.1) | copy-start | bytes 221188
  2.2 15.8 %copy-start.2 = (bf16[2,64,128]{2,1,0:T(8,128)(2,1)S(1)}, bf16[2,64,128]{2,1,0:T(8,128)(2,1)}, u32[]{:S(2)}) copy-start(bf16[2,64,128]{2,1,0:T(8,128)(2,1)} %wq_ref.1) | copy-start | bytes 98308
  2.2 15.8 %copy-start.3 = (bf16[2,64,128]{2,1,0:T(8,128)(2,1)S(1)}, bf16[2,64,128]{2,1,0:T(8,128)(2,1)}, u32[]{:S(2)}) copy-start(bf16[2,64,128]{2,1,0:T(8,128)(2,1)} %wk_ref.1) | copy-start | bytes 98308
  2.2 15.8 %copy-start.4 = (bf16[2,64,128]{2,1,0:T(8,128)(2,1)S(1)}, bf16[2,64,128]{2,1,0:T(8,128)(2,1)}, u32[]{:S(2)}) copy-start(bf16[2,64,128]{2,1,0:T(8,128)(2,1)} %wv_ref.1) | copy-start | bytes 98308

commit v5 on v4

--- a/solution.py
+++ b/solution.py
@@ -37,12 +37,6 @@
     return (centre * lax.rsqrt(spread + 1e-05)).astype(BF16)
 
 
-def folded_values(value_matrix, flipped):
-    return lax.dot_general(
-        value_matrix, flipped, (((1,), (1,)), ((), ())), preferred_element_type=F32
-    ).astype(BF16)
-
-
 def both_halves(*parts):
     lower, upper = [], []
     for first, second in parts:
@@ -53,52 +47,46 @@
     )
 
 
-def exponents(queries, keys, scaling):
-    scores = lax.dot_general(
-        queries, keys, (((1,), (1,)), ((), ())), preferred_element_type=F32
-    )
-    top = jnp.max(scores, axis=-1, keepdims=True)
-    return jnp.exp((scores - top) * scaling).astype(BF16)
-
-
-def weigh(low, high, values):
-    rows, lanes = low.shape[0], values.shape[1] // 2
-    summed = jnp.dot(
-        jnp.concatenate([low, high], axis=0), values, preferred_element_type=F32
-    )
-    lane = lax.broadcasted_iota(jnp.int32, (rows, 2 * lanes), 1) % lanes
-    chosen = jnp.where(lane < lanes // 2, summed[:rows], summed[rows:])
-    return chosen[:, :lanes] / chosen[:, lanes:]
-
-
-def attend_pair(low, high, keys, values, scaling, pieces, mixed):
-    count = low.shape[0]
-    values = jnp.concatenate([values, jnp.ones_like(values)], axis=1)
+def blend(queries, keys, values, scaling):
+    scores = (
+        lax.dot_general(keys, queries, (((1,), (1,)), ((), ())), preferred_element_type=F32)
+        * scaling
+    )
+    exponent = jnp.exp(scores - jnp.max(scores, axis=0, keepdims=True))
+    weights = exponent * (1.0 / jnp.sum(exponent, axis=0, keepdims=True))
+    return jnp.dot(values, weights.astype(BF16), preferred_element_type=F32).astype(BF16)
+
+
+def in_blocks(count, attend, queries, pieces, mixed):
     if count <= QUERY_BLOCK:
-        if len(keys) == 1:
-            both = exponents(jnp.concatenate([low, high], axis=0), keys[0], scaling)
-            return weigh(both[:count], both[count:], values)
-        return weigh(
-            exponents(low, keys[0], scaling), exponents(high, keys[1], scaling), values
-        )
-    width = low.shape[1]
-    key_count = values.shape[0]
-    for index, part in enumerate([low, high]):
+        return attend(*queries)
+    for index, part in enumerate(queries):
         pieces[index, :count] = part
-    for index, part in enumerate([keys[0], keys[-1], values[:, :width], values[:, width:]]):
-        pieces[2 + index, :key_count] = part
 
     def block(index, carry):
         rows = pl.ds(pl.multiple_of(index * QUERY_BLOCK, QUERY_BLOCK), QUERY_BLOCK)
-        mixed[rows, :] = weigh(
-            exponents(pieces[0, rows, :], pieces[2, :key_count], scaling),
-            exponents(pieces[1, rows, :], pieces[3, :key_count], scaling),
-            jnp.concatenate([pieces[4, :key_count], pieces[5, :key_count]], axis=1),
-        )
+        mixed[rows, :] = attend(pieces[0, rows, :], pieces[1, rows, :])
         return carry
 
     lax.fori_loop(0, count // QUERY_BLOCK, block, 0)
     return mixed[:count]
+
+
+def out_halves(flipped):
+    nothing = jnp.zeros_like(flipped)
+    return jnp.concatenate(
+        [
+            jnp.concatenate([flipped, nothing], axis=1),
+            jnp.concatenate([nothing, flipped], axis=1),
+        ],
+        axis=0,
+    )
+
+
+def turned(matrix, normed):
+    return lax.dot_general(
+        matrix, normed, (((0,), (1,)), ((), ())), preferred_element_type=F32
+    ).astype(BF16)
 
 
 def rows_kernel(
@@ -155,36 +143,41 @@
     normed = packed_norm(tokens, channels)
     for copy in copies[1:]:
         copy.wait()
-    query_matrix, key_matrix = wq_ref[...], wk_ref[...]
-    folded = folded_values(wv_ref[...], wo_ref[...])
-    projected = jnp.dot(
-        normed,
-        both_halves(
-            (query_matrix, None),
-            (key_matrix, None),
-            (folded, None),
-            (folded, None),
-            (None, query_matrix),
-            (None, key_matrix),
-            (None, folded),
-            (None, folded),
-        ),
-        preferred_element_type=F32,
-    ).astype(BF16)
-    part = 2 * width + lanes
+    swapped = jnp.concatenate([normed[:, channels:], normed[:, :channels]], axis=1)
+    every = jnp.concatenate(
+        [
+            part[v * per_line : (v + 1) * per_line]
+            for v in range(local_v)
+            for part in (normed, swapped)
+        ],
+        axis=0,
+    )
+    nothing = jnp.zeros((channels, width), BF16)
+    queries, keys = (
+        jnp.dot(
+            every, jnp.concatenate([matrix, nothing], axis=0), preferred_element_type=F32
+        ).astype(BF16)
+        for matrix in (wq_ref[...], wk_ref[...])
+    )
+    values = turned(jnp.concatenate([wv_ref[...], nothing], axis=0), every)
+    out_matrix = jnp.concatenate([wo_ref[...], wo_ref[...]], axis=0)
+    lane = lax.broadcasted_iota(jnp.int32, (min(per_line, QUERY_BLOCK), lanes), 1)
     place = lax.broadcasted_iota(jnp.int32, (owners, lanes), 0) % (pairs // own)
     for v in range(local_v):
         span = slice(v * per_line, (v + 1) * per_line)
-        both = jnp.concatenate([projected[span, :part], projected[span, part:]], axis=0)
-        summed = tokens[span] + attend_pair(
-            both[:per_line, :width],
-            both[per_line:, :width],
-            [both[:, width : 2 * width]],
-            both[:, 2 * width :],
-            scaling,
-            lines,
-            mixed,
-        )
+        line = slice(2 * v * per_line, 2 * (v + 1) * per_line)
+
+        def attend(low, high, line=line):
+            blended = blend(
+                jnp.concatenate([low, high], axis=0), keys[line], values[:, line], scaling
+            )
+            terms = jnp.dot(out_matrix, blended, preferred_element_type=F32).T
+            return jnp.where(
+                lane < channels, terms[: low.shape[0]], terms[low.shape[0] :]
+            )
+
+        halves = [queries[line][:per_line], queries[line][per_line:]]
+        summed = tokens[span] + in_blocks(per_line, attend, halves, lines, mixed)
         spread[v, pl.ds(SUBLANES, per_line), :] = summed
         for step in range(window):
             piece = spread[v, pl.ds(SUBLANES - 1 + step, owners, stride=own), :]
@@ -256,33 +249,30 @@
         [held[pl.ds(step, per_line, stride=window), :] for step in range(window)], axis=0
     )
     normed = packed_norm(tokens, channels)
-    query_matrix, key_matrix = wq_ref[1], wk_ref[1]
-    folded = folded_values(wv_ref[1], wo_ref[1])
+    matrices = [wq_ref[1], wk_ref[1]]
     projected = jnp.dot(
         normed,
-        both_halves(
-            (query_matrix, None),
-            (key_matrix, None),
-            (None, query_matrix),
-            (None, key_matrix),
-            (folded, None),
-            (None, folded),
-        ),
+        both_halves(*[(m, None) for m in matrices], *[(None, m) for m in matrices]),
         preferred_element_type=F32,
     ).astype(BF16)
+    values = turned(both_halves((wv_ref[1], None), (None, wv_ref[1])), normed)
+    out_matrix = out_halves(wo_ref[1])
     images = []
     for step in range(window):
         span = slice(step * per_line, (step + 1) * per_line)
-        queries_keys = [projected[span, i * width : (i + 1) * width] for i in range(4)]
-        summed = tokens[span] + attend_pair(
-            queries_keys[0],
-            queries_keys[2],
-            queries_keys[1::2],
-            projected[span, 4 * width :],
-            scaling,
-            lines,
-            mixed,
-        )
+        parts = [projected[span, i * width : (i + 1) * width] for i in range(4)]
+
+        def attend(low, high, parts=parts, span=span):
+            blended = jnp.concatenate(
+                [
+                    blend(low, parts[1], values[:width, span], scaling),
+                    blend(high, parts[3], values[width:, span], scaling),
+                ],
+                axis=0,
+            )
+            return jnp.dot(out_matrix, blended, preferred_element_type=F32).T
+
+        summed = tokens[span] + in_blocks(per_line, attend, parts[::2], lines, mixed)
         images.append(summed.astype(BF16))
 
     blank = jnp.zeros_like(images[0])
@@ -333,7 +323,7 @@
 
     def scratch(tokens):
         kept = tokens if tokens > QUERY_BLOCK else 16
-        return [pltpu.VMEM((6, kept, width), BF16), pltpu.VMEM((kept, lanes), F32)]
+        return [pltpu.VMEM((2, kept, width), BF16), pltpu.VMEM((kept, lanes), F32)]
 
     leaving = pl.pallas_call(
         rows_kernel,

time: 29.5 us -> 30.6 us (1.037)
  Pallas kernels: 4.2 us -> 5.29 us
    pallas_call x1, Pallas kernels: 1.4 us -> 2.02 us  [local(): pl.pallas_call(functools.partial(columns_kernel, local_v=local_v, views=v...]
    pallas_call x1, Pallas kernels: 2.14 us -> 2.6 us  [local(): pl.pallas_call(rows_kernel, out_shape=jax.ShapeDtypeStruct((devices, loca...]
where the time goes in v5:
time: 30.6 us; the launch traced here: 30.4 us
  blocking collectives  25 us (82%)
  Pallas kernels  5.29 us (17%)
    all_to_all x1, blocking collectives, local(): lax.all_to_all(leaving, AXES, split_axis=0, concat_axis=0, tiled=True)  15.7 us
    all_to_all x1, blocking collectives, local(): lax.all_to_all(finished, AXES, split_axis=0, concat_axis=0, tiled=True)  9.3 us
    pallas_call x1, Pallas kernels, local(): pl.pallas_call(rows_kernel, out_shape=jax.ShapeDtypeStruct((devices, loca...  2.6 us
    pallas_call x1, Pallas kernels, local(): pl.pallas_call(functools.partial(columns_kernel, local_v=local_v, views=v...  2.02 us
    pallas_call x1, Pallas kernels, local(): pl.pallas_call(place_kernel, out_shape=jax.ShapeDtypeStruct((all_u, local...  0.67 us

profile of v5, /device:TPU:0, one launch (start us, length us, event | category | flops | bytes accessed | tf_op | source)
XLA Modules:
  0.0 30.4 jit_solution(10113595520116386038)
XLA Ops:
  0.0 0.0 copy-start.1
  0.0 0.0 copy-start.5
  0.0 2.6 %rows.1 = bf16[32,16,128]{2,1,0:T(8,128)(2,1)S(1)} custom-call(bf16[1,8,4,1024]{3,2,1,0:T(4,128)(2,1)} %x_hbm.1, bf16[2,64,128]{2,1,0:T(8,128)(2,1)} %wq_ref.1, bf16[2,64,128]{2,1,0:T(8,128)(2,1)} %wk_ref.1, bf16[2,64,128]{2,1,0:T(8,128)(2,1)} %wv_ref.1, bf16[2,64,128]{2,1,0:T(8,128)(2,1)} %bitcast.2), custom_call_target="tpu_custom_call" | custom-call | tf_op jit(solution)/shard_map/rows/pallas_call | solution.py:328
  2.6 0.0 copy-start
  2.6 0.0 copy-start.2
  2.6 0.0 copy-start.3
  2.7 0.0 copy-start.4
  2.7 15.7 %all_to_all.10.x_ref = bf16[32,16,128]{2,1,0:T(8,128)(2,1)S(1)} all-to-all(bf16[32,16,128]{2,1,0:T(8,128)(2,1)S(1)} %rows.1), channel_id=1, replica_groups=mesh['line'=16,'view'=2] {'line','view'}, dimensions={0} | all-to-all | bytes 262144 | tf_op jit(solution)/shard_map/all_to_all | solution.py:344
  18.4 0.0 copy-done.1
  18.4 0.0 copy-done.5
  18.4 0.0 copy-done
  18.4 0.0 copy-done.2
  18.4 0.0 copy-done.3
  18.4 0.0 copy-done.4
  18.4 2.0 %columns.1 = bf16[32,8,128]{2,1,0:T(8,128)(2,1)S(1)} custom-call(bf16[32,16,128]{2,1,0:T(8,128)(2,1)S(1)} %all_to_all.10.x_ref, bf16[2,64,128]{2,1,0:T(8,128)(2,1)S(1)} %copy-done.2, bf16[2,64,128]{2,1,0:T(8,128)(2,1)S(1)} %copy-done.3, bf16[2,64,128]{2,1,0:T(8,128)(2,1)S(1)} %copy-done.4, bf16[2,64,128]{2,1,0:T(8,128)(2,1)S(1)} %bitcast.3, ...), custom_call_target="tpu_custom_call" | custom-call | tf_op jit(solution)/shard_map/columns/pallas_call | solution.py:345
  20.5 9.3 %all_to_all.11.x_ref = bf16[32,8,128]{2,1,0:T(8,128)(2,1)S(1)} all-to-all(bf16[32,8,128]{2,1,0:T(8,128)(2,1)S(1)} %columns.1), channel_id=1, replica_groups=mesh['line'=16,'view'=2] {'line','view'}, dimensions={0} | all-to-all | bytes 131072 | tf_op jit(solution)/shard_map/all_to_all | solution.py:356
  29.8 0.7 %place.1 = bf16[8,4,1024]{2,1,0:T(4,128)(2,1)} custom-call(bf16[32,8,128]{2,1,0:T(8,128)(2,1)S(1)} %all_to_all.11.x_ref), custom_call_target="tpu_custom_call" | custom-call | tf_op jit(solution)/shard_map/place/pallas_call | solution.py:357
Async XLA Ops:
  0.0 18.4 %copy-start.1 = (bf16[3,3,64,64]{3,2,1,0:T(8,128)(2,1)S(1)}, bf16[3,3,64,64]{3,2,1,0:T(8,128)(2,1)}, u32[]{:S(2)}) copy-start(bf16[3,3,64,64]{3,2,1,0:T(8,128)(2,1)} %second_ref.1) | copy-start | bytes 221188
  0.0 18.4 %copy-start.5 = (bf16[2,128,64]{1,2,0:T(8,128)(2,1)S(1)}, bf16[2,128,64]{1,2,0:T(8,128)(2,1)}, u32[]{:S(2)}) copy-start(bf16[2,128,64]{1,2,0:T(8,128)(2,1)} %param.11) | copy-start | bytes 98308
  2.6 15.8 %copy-start = (bf16[3,3,64,64]{3,2,1,0:T(8,128)(2,1)S(1)}, bf16[3,3,64,64]{3,2,1,0:T(8,128)(2,1)}, u32[]{:S(2)}) copy-start(bf16[3,3,64,64]{3,2,1,0:T(8,128)(2,1)} %first_ref.1) | copy-start | bytes 221188
  2.6 15.8 %copy-start.2 = (bf16[2,64,128]{2,1,0:T(8,128)(2,1)S(1)}, bf16[2,64,128]{2,1,0:T(8,128)(2,1)}, u32[]{:S(2)}) copy-start(bf16[2,64,128]{2,1,0:T(8,128)(2,1)} %wq_ref.1) | copy-start | bytes 98308
  2.6 15.8 %copy-start.3 = (bf16[2,64,128]{2,1,0:T(8,128)(2,1)S(1)}, bf16[2,64,128]{2,1,0:T(8,128)(2,1)}, u32[]{:S(2)}) copy-start(bf16[2,64,128]{2,1,0:T(8,128)(2,1)} %wk_ref.1) | copy-start | bytes 98308
  2.7 15.8 %copy-start.4 = (bf16[2,64,128]{2,1,0:T(8,128)(2,1)S(1)}, bf16[2,64,128]{2,1,0:T(8,128)(2,1)}, u32[]{:S(2)}) copy-start(bf16[2,64,128]{2,1,0:T(8,128)(2,1)} %wv_ref.1) | copy-start | bytes 98308

commit v6 on v5

--- a/solution.py
+++ b/solution.py
@@ -47,29 +47,47 @@
     )
 
 
-def blend(queries, keys, values, scaling):
-    scores = (
+def score(queries, keys, scaling):
+    return (
         lax.dot_general(keys, queries, (((1,), (1,)), ((), ())), preferred_element_type=F32)
         * scaling
     )
+
+
+def soften(scores):
     exponent = jnp.exp(scores - jnp.max(scores, axis=0, keepdims=True))
-    weights = exponent * (1.0 / jnp.sum(exponent, axis=0, keepdims=True))
-    return jnp.dot(values, weights.astype(BF16), preferred_element_type=F32).astype(BF16)
-
-
-def in_blocks(count, attend, queries, pieces, mixed):
+    return (exponent * (1.0 / jnp.sum(exponent, axis=0, keepdims=True))).astype(BF16)
+
+
+def blend(lines, values, scaling):
+    values = values()
+    scores = [score(queries, keys, scaling) for queries, keys in lines]
+    weights = [soften(part) for part in scores]
+    return [
+        jnp.dot(part, weight, preferred_element_type=F32).astype(BF16)
+        for part, weight in zip(values, weights)
+    ]
+
+
+def in_blocks(count, attend, lines, values, pieces, mixed):
     if count <= QUERY_BLOCK:
-        return attend(*queries)
-    for index, part in enumerate(queries):
-        pieces[index, :count] = part
-
-    def block(index, carry):
-        rows = pl.ds(pl.multiple_of(index * QUERY_BLOCK, QUERY_BLOCK), QUERY_BLOCK)
-        mixed[rows, :] = attend(pieces[0, rows, :], pieces[1, rows, :])
-        return carry
-
-    lax.fori_loop(0, count // QUERY_BLOCK, block, 0)
-    return mixed[:count]
+        return attend(lines, values)
+    values, results = values(), []
+    for low, high, keys in lines:
+        own_values = values[: len(keys)]
+        values = values[len(keys) :]
+        for index, part in enumerate([low, high]):
+            pieces[index, :count] = part
+
+        def block(index, carry, keys=keys, own_values=own_values):
+            rows = pl.ds(pl.multiple_of(index * QUERY_BLOCK, QUERY_BLOCK), QUERY_BLOCK)
+            line = (pieces[0, rows, :], pieces[1, rows, :], keys)
+            (mixed[rows, :],) = attend([line], lambda: own_values)
+            return carry
+
+        lax.fori_loop(0, count // QUERY_BLOCK, block, 0)
+        results.append(mixed[:count])
+    return results
 
 
 def out_halves(flipped):
@@ -80,6 +98,12 @@
             jnp.concatenate([nothing, flipped], axis=1),
         ],
         axis=0,
+    )
+
+
+def project_out(blended, out_matrix):
+    return lax.dot_general(
+        blended, out_matrix, (((0,), (1,)), ((), ())), preferred_element_type=F32
     )
 
 
@@ -130,7 +154,8 @@
     window = chunk // local_v
     own = window - 2
     scaling = 1.0 / math.sqrt(width)
-    copies[0].wait()
+    for copy in copies:
+        copy.wait()
     for u in range(all_u):
         rows = x_ref[u].astype(F32)
         for pair in range(pairs):
@@ -141,8 +166,6 @@
         [held[pl.ds(v, per_line, stride=local_v), :] for v in range(local_v)], axis=0
     )
     normed = packed_norm(tokens, channels)
-    for copy in copies[1:]:
-        copy.wait()
     swapped = jnp.concatenate([normed[:, channels:], normed[:, :channels]], axis=1)
     every = jnp.concatenate(
         [
@@ -159,26 +182,34 @@
         ).astype(BF16)
         for matrix in (wq_ref[...], wk_ref[...])
     )
-    values = turned(jnp.concatenate([wv_ref[...], nothing], axis=0), every)
     out_matrix = jnp.concatenate([wo_ref[...], wo_ref[...]], axis=0)
     lane = lax.broadcasted_iota(jnp.int32, (min(per_line, QUERY_BLOCK), lanes), 1)
     place = lax.broadcasted_iota(jnp.int32, (owners, lanes), 0) % (pairs // own)
+
+    def attend(entries, values):
+        blended = blend(
+            [(jnp.concatenate([low, high], axis=0), *keys) for low, high, keys in entries],
+            values,
+            scaling,
+        )
+        terms = [project_out(part, out_matrix) for part in blended]
+        half = lane.shape[0]
+        return [jnp.where(lane < channels, term[:half], term[half:]) for term in terms]
+
+    def flipped_values():
+        whole = turned(jnp.concatenate([wv_ref[...], nothing], axis=0), every)
+        return [whole[:, 2 * v * per_line : 2 * (v + 1) * per_line] for v in range(local_v)]
+
+    entries = []
     for v in range(local_v):
+        low = slice(2 * v * per_line, (2 * v + 1) * per_line)
+        high = slice((2 * v + 1) * per_line, 2 * (v + 1) * per_line)
+        line = slice(2 * v * per_line, 2 * (v + 1) * per_line)
+        entries.append((queries[low], queries[high], [keys[line]]))
+    results = in_blocks(per_line, attend, entries, flipped_values, lines, mixed)
+    for v, terms in enumerate(results):
         span = slice(v * per_line, (v + 1) * per_line)
-        line = slice(2 * v * per_line, 2 * (v + 1) * per_line)
-
-        def attend(low, high, line=line):
-            blended = blend(
-                jnp.concatenate([low, high], axis=0), keys[line], values[:, line], scaling
-            )
-            terms = jnp.dot(out_matrix, blended, preferred_element_type=F32).T
-            return jnp.where(
-                lane < channels, terms[: low.shape[0]], terms[low.shape[0] :]
-            )
-
-        halves = [queries[line][:per_line], queries[line][per_line:]]
-        summed = tokens[span] + in_blocks(per_line, attend, halves, lines, mixed)
-        spread[v, pl.ds(SUBLANES, per_line), :] = summed
+        spread[v, pl.ds(SUBLANES, per_line), :] = tokens[span] + terms
         for step in range(window):
             piece = spread[v, pl.ds(SUBLANES - 1 + step, owners, stride=own), :]
             if step == 0:
@@ -255,25 +286,37 @@
         both_halves(*[(m, None) for m in matrices], *[(None, m) for m in matrices]),
         preferred_element_type=F32,
     ).astype(BF16)
-    values = turned(both_halves((wv_ref[1], None), (None, wv_ref[1])), normed)
     out_matrix = out_halves(wo_ref[1])
-    images = []
-    for step in range(window):
-        span = slice(step * per_line, (step + 1) * per_line)
+
+    def attend(entries, values):
+        blended = blend(
+            [
+                line
+                for low, high, keys in entries
+                for line in ((low, keys[0]), (high, keys[1]))
+            ],
+            values,
+            scaling,
+        )
+        return [
+            project_out(jnp.concatenate(pair, axis=0), out_matrix)
+            for pair in zip(blended[::2], blended[1::2])
+        ]
+
+    spans = [slice(step * per_line, (step + 1) * per_line) for step in range(window)]
+
+    def flipped_values():
+        whole = turned(both_halves((wv_ref[1], None), (None, wv_ref[1])), normed)
+        return [
+            whole[half * width : (half + 1) * width, span] for span in spans for half in range(2)
+        ]
+
+    entries = []
+    for span in spans:
         parts = [projected[span, i * width : (i + 1) * width] for i in range(4)]
-
-        def attend(low, high, parts=parts, span=span):
-            blended = jnp.concatenate(
-                [
-                    blend(low, parts[1], values[:width, span], scaling),
-                    blend(high, parts[3], values[width:, span], scaling),
-                ],
-                axis=0,
-            )
-            return jnp.dot(out_matrix, blended, preferred_element_type=F32).T
-
-        summed = tokens[span] + in_blocks(per_line, attend, parts[::2], lines, mixed)
-        images.append(summed.astype(BF16))
+        entries.append((*parts[::2], parts[1::2]))
+    results = in_blocks(per_line, attend, entries, flipped_values, lines, mixed)
+    images = [(tokens[span] + terms).astype(BF16) for span, terms in zip(spans, results)]
 
     blank = jnp.zeros_like(images[0])
     hidden = [

time: 30.6 us -> 29.6 us (0.967)
  Pallas kernels: 5.29 us -> 4.26 us
    pallas_call x1, Pallas kernels: 2.6 us -> 2.05 us  [local(): pl.pallas_call(rows_kernel, out_shape=jax.ShapeDtypeStruct((devices, loca...]
    pallas_call x1, Pallas kernels: 2.02 us -> 1.53 us  [local(): pl.pallas_call(functools.partial(columns_kernel, local_v=local_v, views=v...]
where the time goes in v6:
time: 29.6 us; the launch traced here: 29.4 us
  blocking collectives  25 us (84%)
  Pallas kernels  4.26 us (14%)
    all_to_all x1, blocking collectives, local(): lax.all_to_all(leaving, AXES, split_axis=0, concat_axis=0, tiled=True)  15.7 us
    all_to_all x1, blocking collectives, local(): lax.all_to_all(finished, AXES, split_axis=0, concat_axis=0, tiled=True)  9.3 us
    pallas_call x1, Pallas kernels, local(): pl.pallas_call(rows_kernel, out_shape=jax.ShapeDtypeStruct((devices, loca...  2.05 us
    pallas_call x1, Pallas kernels, local(): pl.pallas_call(functools.partial(columns_kernel, local_v=local_v, views=v...  1.53 us
    pallas_call x1, Pallas kernels, local(): pl.pallas_call(place_kernel, out_shape=jax.ShapeDtypeStruct((all_u, local...  0.67 us

profile of v6, /device:TPU:0, one launch (start us, length us, event | category | flops | bytes accessed | tf_op | source)
XLA Modules:
  0.0 29.4 jit_solution(6257274422908524591)
XLA Ops:
  0.0 0.0 copy-start.1
  0.0 0.0 copy-start.5
  0.0 2.1 %rows.1 = bf16[32,16,128]{2,1,0:T(8,128)(2,1)S(1)} custom-call(bf16[1,8,4,1024]{3,2,1,0:T(4,128)(2,1)} %x_hbm.1, bf16[2,64,128]{2,1,0:T(8,128)(2,1)} %wq_ref.1, bf16[2,64,128]{2,1,0:T(8,128)(2,1)} %wk_ref.1, bf16[2,64,128]{2,1,0:T(8,128)(2,1)} %wv_ref.1, bf16[2,64,128]{2,1,0:T(8,128)(2,1)} %bitcast.2), custom_call_target="tpu_custom_call" | custom-call | tf_op jit(solution)/shard_map/rows/pallas_call | solution.py:371
  2.1 0.0 copy-start
  2.1 0.0 copy-start.2
  2.1 0.0 copy-start.3
  2.1 0.0 copy-start.4
  2.1 15.7 %all_to_all.10.x_ref = bf16[32,16,128]{2,1,0:T(8,128)(2,1)S(1)} all-to-all(bf16[32,16,128]{2,1,0:T(8,128)(2,1)S(1)} %rows.1), channel_id=1, replica_groups=mesh['line'=16,'view'=2] {'line','view'}, dimensions={0} | all-to-all | bytes 262144 | tf_op jit(solution)/shard_map/all_to_all | solution.py:387
  17.9 0.0 copy-done.1
  17.9 0.0 copy-done.5
  17.9 0.0 copy-done
  17.9 0.0 copy-done.2
  17.9 0.0 copy-done.3
  17.9 0.0 copy-done.4
  17.9 1.5 %columns.1 = bf16[32,8,128]{2,1,0:T(8,128)(2,1)S(1)} custom-call(bf16[32,16,128]{2,1,0:T(8,128)(2,1)S(1)} %all_to_all.10.x_ref, bf16[2,64,128]{2,1,0:T(8,128)(2,1)S(1)} %copy-done.2, bf16[2,64,128]{2,1,0:T(8,128)(2,1)S(1)} %copy-done.3, bf16[2,64,128]{2,1,0:T(8,128)(2,1)S(1)} %copy-done.4, bf16[2,64,128]{2,1,0:T(8,128)(2,1)S(1)} %bitcast.3, ...), custom_call_target="tpu_custom_call" | custom-call | tf_op jit(solution)/shard_map/columns/pallas_call | solution.py:388
  19.4 9.3 %all_to_all.11.x_ref = bf16[32,8,128]{2,1,0:T(8,128)(2,1)S(1)} all-to-all(bf16[32,8,128]{2,1,0:T(8,128)(2,1)S(1)} %columns.1), channel_id=1, replica_groups=mesh['line'=16,'view'=2] {'line','view'}, dimensions={0} | all-to-all | bytes 131072 | tf_op jit(solution)/shard_map/all_to_all | solution.py:399
  28.7 0.7 %place.1 = bf16[8,4,1024]{2,1,0:T(4,128)(2,1)} custom-call(bf16[32,8,128]{2,1,0:T(8,128)(2,1)S(1)} %all_to_all.11.x_ref), custom_call_target="tpu_custom_call" | custom-call | tf_op jit(solution)/shard_map/place/pallas_call | solution.py:400
Async XLA Ops:
  0.0 17.9 %copy-start.1 = (bf16[3,3,64,64]{3,2,1,0:T(8,128)(2,1)S(1)}, bf16[3,3,64,64]{3,2,1,0:T(8,128)(2,1)}, u32[]{:S(2)}) copy-start(bf16[3,3,64,64]{3,2,1,0:T(8,128)(2,1)} %second_ref.1) | copy-start | bytes 221188
  0.0 17.9 %copy-start.5 = (bf16[2,128,64]{1,2,0:T(8,128)(2,1)S(1)}, bf16[2,128,64]{1,2,0:T(8,128)(2,1)}, u32[]{:S(2)}) copy-start(bf16[2,128,64]{1,2,0:T(8,128)(2,1)} %param.11) | copy-start | bytes 98308
  2.1 15.8 %copy-start = (bf16[3,3,64,64]{3,2,1,0:T(8,128)(2,1)S(1)}, bf16[3,3,64,64]{3,2,1,0:T(8,128)(2,1)}, u32[]{:S(2)}) copy-start(bf16[3,3,64,64]{3,2,1,0:T(8,128)(2,1)} %first_ref.1) | copy-start | bytes 221188
  2.1 15.8 %copy-start.2 = (bf16[2,64,128]{2,1,0:T(8,128)(2,1)S(1)}, bf16[2,64,128]{2,1,0:T(8,128)(2,1)}, u32[]{:S(2)}) copy-start(bf16[2,64,128]{2,1,0:T(8,128)(2,1)} %wq_ref.1) | copy-start | bytes 98308
  2.1 15.8 %copy-start.3 = (bf16[2,64,128]{2,1,0:T(8,128)(2,1)S(1)}, bf16[2,64,128]{2,1,0:T(8,128)(2,1)}, u32[]{:S(2)}) copy-start(bf16[2,64,128]{2,1,0:T(8,128)(2,1)} %wk_ref.1) | copy-start | bytes 98308
  2.1 15.8 %copy-start.4 = (bf16[2,64,128]{2,1,0:T(8,128)(2,1)S(1)}, bf16[2,64,128]{2,1,0:T(8,128)(2,1)}, u32[]{:S(2)}) copy-start(bf16[2,64,128]{2,1,0:T(8,128)(2,1)} %wv_ref.1) | copy-start | bytes 98308

commit v7 on v6

--- a/solution.py
+++ b/solution.py
@@ -8,7 +8,7 @@
 from jax.experimental.pallas import tpu as pltpu
 from jax.sharding import PartitionSpec as P
 
-AXES = ("line", "view")
+AXES = ("view", "line")
 QUERY_BLOCK = 256
 F32 = jnp.float32
 BF16 = jnp.bfloat16
@@ -60,8 +60,8 @@
 
 
 def blend(lines, values, scaling):
+    scores = [score(queries, keys, scaling) for queries, keys in lines]
     values = values()
-    scores = [score(queries, keys, scaling) for queries, keys in lines]
     weights = [soften(part) for part in scores]
     return [
         jnp.dot(part, weight, preferred_element_type=F32).astype(BF16)
@@ -166,22 +166,12 @@
         [held[pl.ds(v, per_line, stride=local_v), :] for v in range(local_v)], axis=0
     )
     normed = packed_norm(tokens, channels)
-    swapped = jnp.concatenate([normed[:, channels:], normed[:, :channels]], axis=1)
-    every = jnp.concatenate(
-        [
-            part[v * per_line : (v + 1) * per_line]
-            for v in range(local_v)
-            for part in (normed, swapped)
-        ],
-        axis=0,
-    )
-    nothing = jnp.zeros((channels, width), BF16)
-    queries, keys = (
-        jnp.dot(
-            every, jnp.concatenate([matrix, nothing], axis=0), preferred_element_type=F32
-        ).astype(BF16)
-        for matrix in (wq_ref[...], wk_ref[...])
-    )
+    matrices = [wq_ref[...], wk_ref[...]]
+    projected = jnp.dot(
+        normed,
+        both_halves(*[(m, None) for m in matrices], *[(None, m) for m in matrices]),
+        preferred_element_type=F32,
+    ).astype(BF16)
     out_matrix = jnp.concatenate([wo_ref[...], wo_ref[...]], axis=0)
     lane = lax.broadcasted_iota(jnp.int32, (min(per_line, QUERY_BLOCK), lanes), 1)
     place = lax.broadcasted_iota(jnp.int32, (owners, lanes), 0) % (pairs // own)
@@ -197,15 +187,24 @@
         return [jnp.where(lane < channels, term[:half], term[half:]) for term in terms]
 
     def flipped_values():
-        whole = turned(jnp.concatenate([wv_ref[...], nothing], axis=0), every)
+        swapped = jnp.concatenate([normed[:, channels:], normed[:, :channels]], axis=1)
+        every = jnp.concatenate(
+            [
+                part[v * per_line : (v + 1) * per_line]
+                for v in range(local_v)
+                for part in (normed, swapped)
+            ],
+            axis=0,
+        )
+        padded = jnp.concatenate([wv_ref[...], jnp.zeros_like(wv_ref[...])], axis=0)
+        whole = turned(padded, every)
         return [whole[:, 2 * v * per_line : 2 * (v + 1) * per_line] for v in range(local_v)]
 
     entries = []
     for v in range(local_v):
-        low = slice(2 * v * per_line, (2 * v + 1) * per_line)
-        high = slice((2 * v + 1) * per_line, 2 * (v + 1) * per_line)
-        line = slice(2 * v * per_line, 2 * (v + 1) * per_line)
-        entries.append((queries[low], queries[high], [keys[line]]))
+        span = slice(v * per_line, (v + 1) * per_line)
+        parts = [projected[span, i * width : (i + 1) * width] for i in range(4)]
+        entries.append((*parts[::2], [jnp.concatenate(parts[1::2], axis=0)]))
     results = in_blocks(per_line, attend, entries, flipped_values, lines, mixed)
     for v, terms in enumerate(results):
         span = slice(v * per_line, (v + 1) * per_line)
@@ -260,7 +259,6 @@
     second_ref,
     o_ref,
     held,
-    leaving,
     lines,
     mixed,
     *,
@@ -275,7 +273,10 @@
     per_line = sources * local_v
     row = views * local_v
     scaling = 1.0 / math.sqrt(width)
-    held[...] = x_ref[...].astype(F32).reshape(held.shape)
+    rows = sources // views
+    slots = [source % rows * views + source // rows for source in range(sources)]
+    for source, slot in enumerate(slots):
+        held[pl.ds(slot * chunk, chunk), :] = x_ref[source].astype(F32)
     tokens = jnp.concatenate(
         [held[pl.ds(step, per_line, stride=window), :] for step in range(window)], axis=0
     )
@@ -323,28 +324,14 @@
         jnp.where(value >= 0, value, 0.1 * value)
         for value in correlate([blank, *images, blank], pair_weights(first_ref[...]), row)
     ]
-    place = (lax.axis_index("line") * views + lax.axis_index("view")) % places
+    place = (lax.axis_index("view") * rows + lax.axis_index("line")) % places
     hidden[0] = jnp.where(place > 0, hidden[0], 0.0)
     hidden[-1] = jnp.where(place < places - 1, hidden[-1], 0.0)
     hidden = [value.astype(BF16) for value in hidden]
     for step, value in enumerate(correlate(hidden, pair_weights(second_ref[...]), row)):
-        leaving[pl.ds(step, per_line, stride=own), :] = images[step + 1].astype(F32) + value
-    o_ref[...] = leaving[...].astype(BF16).reshape(o_ref.shape)
-
-
-def place_kernel(x_ref, o_ref, held):
-    sources, chunk, lanes = x_ref.shape
-    all_u, local_v, packed = o_ref.shape
-    own = chunk // local_v
-    places = sources // all_u
-    held[...] = x_ref[...].astype(F32).reshape(held.shape)
-    for source in range(sources):
-        u, place = source // places, source % places
-        for step in range(own):
-            start = (place * own + step) * lanes
-            o_ref[u, :, start : start + lanes] = held[
-                pl.ds(source * chunk + step, local_v, stride=own), :
-            ].astype(BF16)
+        result = (images[step + 1].astype(F32) + value).astype(BF16)
+        for source, slot in enumerate(slots):
+            o_ref[source * own + step] = result[slot * local_v : (slot + 1) * local_v]
 
 
 def local(light_field, query_weight, key_weight, value_weight, out_weight, conv_first, conv_second):
@@ -387,24 +374,17 @@
     arrived = lax.all_to_all(leaving, AXES, split_axis=0, concat_axis=0, tiled=True)
     finished = pl.pallas_call(
         functools.partial(columns_kernel, local_v=local_v, views=views, places=places),
-        out_shape=jax.ShapeDtypeStruct((devices, local_v * own, lanes), BF16),
+        out_shape=jax.ShapeDtypeStruct((packed_lines, local_v, lanes), BF16),
         scratch_shapes=[
             pltpu.VMEM((devices * local_v * window, lanes), F32),
-            pltpu.VMEM((devices * local_v * own, lanes), F32),
             *scratch(devices * local_v),
         ],
         compiler_params=params,
         name="columns",
     )(arrived, *weights, conv_first, conv_second)
     returned = lax.all_to_all(finished, AXES, split_axis=0, concat_axis=0, tiled=True)
-    result = pl.pallas_call(
-        place_kernel,
-        out_shape=jax.ShapeDtypeStruct((all_u, local_v, packed), BF16),
-        scratch_shapes=[pltpu.VMEM((devices * local_v * own, lanes), F32)],
-        compiler_params=params,
-        name="place",
-    )(returned)
-    return result[None]
+    result = returned.reshape(all_u, pairs, local_v, lanes).transpose(0, 2, 1, 3)
+    return result.reshape(light_field.shape)
 
 
 def solution(mesh):

time: 29.6 us -> 29 us (0.980)
  Pallas kernels: 4.26 us -> 3.6 us
  local copies, waits for them, and re-layouts: 0.03 us -> 0.66 us
  blocking collectives: 25 us -> 24.4 us
    pallas_call x1 -> x0, Pallas kernels: 0.67 us -> none  [local(): pl.pallas_call(place_kernel, out_shape=jax.ShapeDtypeStruct((all_u, local...]
    unnamed x12 -> x13, local copies, waits for them, and re-layouts: 0.03 us -> 0.66 us
    all_to_all x1, blocking collectives: 15.7 us -> 15.3 us  [local(): lax.all_to_all(leaving, AXES, split_axis=0, concat_axis=0, tiled=True)]
where the time goes in v7:
time: 29 us; the launch traced here: 28.8 us
  blocking collectives  24.4 us (84%)
  Pallas kernels  3.6 us (12%)
  local copies, waits for them, and re-layouts  0.66 us (2%)
    all_to_all x1, blocking collectives, local(): lax.all_to_all(leaving, AXES, split_axis=0, concat_axis=0, tiled=True)  15.3 us
    all_to_all x1, blocking collectives, local(): lax.all_to_all(finished, AXES, split_axis=0, concat_axis=0, tiled=True)  9.11 us
    pallas_call x1, Pallas kernels, local(): pl.pallas_call(rows_kernel, out_shape=jax.ShapeDtypeStruct((devices, loca...  2.04 us
    pallas_call x1, Pallas kernels, local(): pl.pallas_call(functools.partial(columns_kernel, local_v=local_v, views=v...  1.56 us
    unnamed x13, local copies, waits for them, and re-layouts  0.66 us

profile of v7, /device:TPU:0, one launch (start us, length us, event | category | flops | bytes accessed | tf_op | source)
XLA Modules:
  0.0 28.8 jit_solution(1052550524609505020)
XLA Ops:
  0.0 0.0 copy-start.1
  0.0 0.0 copy-start.5
  0.0 2.0 %rows.1 = bf16[32,16,128]{2,1,0:T(8,128)(2,1)S(1)} custom-call(bf16[1,8,4,1024]{3,2,1,0:T(4,128)(2,1)} %x_hbm.1, bf16[2,64,128]{2,1,0:T(8,128)(2,1)} %wq_ref.1, bf16[2,64,128]{2,1,0:T(8,128)(2,1)} %wk_ref.1, bf16[2,64,128]{2,1,0:T(8,128)(2,1)} %wv_ref.1, bf16[2,64,128]{2,1,0:T(8,128)(2,1)} %bitcast.6), custom_call_target="tpu_custom_call" | custom-call | tf_op jit(solution)/shard_map/rows/pallas_call | solution.py:358
  2.1 0.0 copy-start
  2.1 0.0 copy-start.2
  2.1 0.0 copy-start.3
  2.1 0.0 copy-start.4
  2.1 15.3 %all_to_all.10.x_ref = bf16[32,16,128]{2,1,0:T(8,128)(2,1)S(1)} all-to-all(bf16[32,16,128]{2,1,0:T(8,128)(2,1)S(1)} %rows.1), channel_id=1, replica_groups=mesh['line'=16,'view'=2] {'view','line'}, dimensions={0} | all-to-all | bytes 262144 | tf_op jit(solution)/shard_map/all_to_all | solution.py:374
  17.4 0.0 copy-done.1
  17.4 0.0 copy-done.5
  17.4 0.0 copy-done
  17.4 0.0 copy-done.2
  17.5 0.0 copy-done.3
  17.5 0.0 copy-done.4
  17.5 1.6 %columns.1 = bf16[64,4,128]{2,1,0:T(4,128)(2,1)S(1)} custom-call(bf16[32,16,128]{2,1,0:T(8,128)(2,1)S(1)} %all_to_all.10.x_ref, bf16[2,64,128]{2,1,0:T(8,128)(2,1)S(1)} %copy-done.2, bf16[2,64,128]{2,1,0:T(8,128)(2,1)S(1)} %copy-done.3, bf16[2,64,128]{2,1,0:T(8,128)(2,1)S(1)} %copy-done.4, bf16[2,64,128]{2,1,0:T(8,128)(2,1)S(1)} %bitcast.7, ...), custom_call_target="tpu_custom_call" | custom-call | tf_op jit(solution)/shard_map/columns/pallas_call | solution.py:375
  19.0 9.1 %all_to_all.11 = bf16[64,4,128]{2,1,0:T(4,128)(2,1)S(1)} all-to-all(bf16[64,4,128]{2,1,0:T(4,128)(2,1)S(1)} %columns.1), channel_id=1, replica_groups=mesh['line'=16,'view'=2] {'view','line'}, dimensions={0} | all-to-all | bytes 131072 | tf_op jit(solution)/shard_map/all_to_all | solution.py:385
  28.2 0.6 %copy.10 = bf16[1,8,4,1024]{3,2,1,0:T(4,128)(2,1)} copy(bf16[1,8,4,1024]{3,2,1,0:T(4,128)(2,1)S(1)} %bitcast.8) | data formatting | bytes 131072
Async XLA Ops:
  0.0 17.4 %copy-start.1 = (bf16[3,3,64,64]{3,2,1,0:T(8,128)(2,1)S(1)}, bf16[3,3,64,64]{3,2,1,0:T(8,128)(2,1)}, u32[]{:S(2)}) copy-start(bf16[3,3,64,64]{3,2,1,0:T(8,128)(2,1)} %second_ref.1) | copy-start | bytes 221188
  0.0 17.4 %copy-start.5 = (bf16[2,128,64]{1,2,0:T(8,128)(2,1)S(1)}, bf16[2,128,64]{1,2,0:T(8,128)(2,1)}, u32[]{:S(2)}) copy-start(bf16[2,128,64]{1,2,0:T(8,128)(2,1)} %param.11) | copy-start | bytes 98308
  2.1 15.4 %copy-start = (bf16[3,3,64,64]{3,2,1,0:T(8,128)(2,1)S(1)}, bf16[3,3,64,64]{3,2,1,0:T(8,128)(2,1)}, u32[]{:S(2)}) copy-start(bf16[3,3,64,64]{3,2,1,0:T(8,128)(2,1)} %first_ref.1) | copy-start | bytes 221188
  2.1 15.4 %copy-start.2 = (bf16[2,64,128]{2,1,0:T(8,128)(2,1)S(1)}, bf16[2,64,128]{2,1,0:T(8,128)(2,1)}, u32[]{:S(2)}) copy-start(bf16[2,64,128]{2,1,0:T(8,128)(2,1)} %wq_ref.1) | copy-start | bytes 98308
  2.1 15.4 %copy-start.3 = (bf16[2,64,128]{2,1,0:T(8,128)(2,1)S(1)}, bf16[2,64,128]{2,1,0:T(8,128)(2,1)}, u32[]{:S(2)}) copy-start(bf16[2,64,128]{2,1,0:T(8,128)(2,1)} %wk_ref.1) | copy-start | bytes 98308
  2.1 15.4 %copy-start.4 = (bf16[2,64,128]{2,1,0:T(8,128)(2,1)S(1)}, bf16[2,64,128]{2,1,0:T(8,128)(2,1)}, u32[]{:S(2)}) copy-start(bf16[2,64,128]{2,1,0:T(8,128)(2,1)} %wv_ref.1) | copy-start | bytes 98308

commit v8 on v7

--- a/solution.py
+++ b/solution.py
@@ -119,7 +119,15 @@
     wk_hbm,
     wv_hbm,
     wo_hbm,
+    first_hbm,
+    second_hbm,
     o_ref,
+    next_wq,
+    next_wk,
+    next_wv,
+    next_wo,
+    next_first,
+    next_second,
     held,
     spread,
     leaving,
@@ -143,7 +151,19 @@
         pltpu.make_async_copy(source.at[0], target, arrivals.at[index])
         for index, (source, target) in enumerate(pulls)
     ]
-    for copy in copies:
+    passed_on = [
+        (wq_hbm.at[1], next_wq),
+        (wk_hbm.at[1], next_wk),
+        (wv_hbm.at[1], next_wv),
+        (wo_hbm.at[1], next_wo),
+        (first_hbm, next_first),
+        (second_hbm, next_second),
+    ]
+    later = [
+        pltpu.make_async_copy(source, target, arrivals.at[len(pulls) + index])
+        for index, (source, target) in enumerate(passed_on)
+    ]
+    for copy in copies + later:
         copy.start()
     all_u, local_v, packed = x_ref.shape
     channels, width = wq_ref.shape
@@ -217,6 +237,8 @@
                 piece = jnp.where(place == pairs // own - 1, 0.0, piece)
             leaving[pl.ds(v * window + step, owners, stride=chunk), :] = piece
     o_ref[...] = leaving[...].astype(BF16).reshape(o_ref.shape)
+    for copy in later:
+        copy.wait()
 
 
 def pair_weights(kernel):
@@ -267,7 +289,7 @@
     places,
 ):
     sources, chunk, lanes = x_ref.shape
-    channels, width = wq_ref.shape[1:]
+    channels, width = wq_ref.shape
     window = chunk // local_v
     own = window - 2
     per_line = sources * local_v
@@ -281,13 +303,13 @@
         [held[pl.ds(step, per_line, stride=window), :] for step in range(window)], axis=0
     )
     normed = packed_norm(tokens, channels)
-    matrices = [wq_ref[1], wk_ref[1]]
+    matrices = [wq_ref[...], wk_ref[...]]
     projected = jnp.dot(
         normed,
         both_halves(*[(m, None) for m in matrices], *[(None, m) for m in matrices]),
         preferred_element_type=F32,
     ).astype(BF16)
-    out_matrix = out_halves(wo_ref[1])
+    out_matrix = out_halves(wo_ref[...])
 
     def attend(entries, values):
         blended = blend(
@@ -307,7 +329,7 @@
     spans = [slice(step * per_line, (step + 1) * per_line) for step in range(window)]
 
     def flipped_values():
-        whole = turned(both_halves((wv_ref[1], None), (None, wv_ref[1])), normed)
+        whole = turned(both_halves((wv_ref[...], None), (None, wv_ref[...])), normed)
         return [
             whole[half * width : (half + 1) * width, span] for span in spans for half in range(2)
         ]
@@ -355,10 +377,16 @@
         kept = tokens if tokens > QUERY_BLOCK else 16
         return [pltpu.VMEM((2, kept, width), BF16), pltpu.VMEM((kept, lanes), F32)]
 
-    leaving = pl.pallas_call(
+    weights = (*weights, conv_first, conv_second)
+    leaving, *later = pl.pallas_call(
         rows_kernel,
-        out_shape=jax.ShapeDtypeStruct((devices, local_v * window, lanes), BF16),
-        in_specs=[pl.BlockSpec(memory_space=pltpu.HBM)] * 5,
+        out_shape=[
+            jax.ShapeDtypeStruct((devices, local_v * window, lanes), BF16),
+            *[jax.ShapeDtypeStruct((channels, width), BF16)] * 4,
+            jax.ShapeDtypeStruct(conv_first.shape, BF16),
+            jax.ShapeDtypeStruct(conv_second.shape, BF16),
+        ],
+        in_specs=[pl.BlockSpec(memory_space=pltpu.HBM)] * 7,
         scratch_shapes=[
             pltpu.VMEM((packed_lines * local_v, lanes), F32),
             pltpu.VMEM((local_v, packed_lines + 2 * SUBLANES, lanes), F32),
@@ -366,7 +394,7 @@
             *scratch(2 * packed_lines),
             pltpu.VMEM((all_u, local_v, packed), BF16),
             *[pltpu.VMEM((channels, width), BF16)] * 4,
-            pltpu.SemaphoreType.DMA((5,)),
+            pltpu.SemaphoreType.DMA((11,)),
         ],
         compiler_params=params,
         name="rows",
@@ -381,7 +409,7 @@
         ],
         compiler_params=params,
         name="columns",
-    )(arrived, *weights, conv_first, conv_second)
+    )(arrived, *later)
     returned = lax.all_to_all(finished, AXES, split_axis=0, concat_axis=0, tiled=True)
     result = returned.reshape(all_u, pairs, local_v, lanes).transpose(0, 2, 1, 3)
     return result.reshape(light_field.shape)

time: 29 us -> 28.9 us (level)
    unnamed x13 -> x1, local copies, waits for them, and re-layouts: 0.66 us -> 0.63 us
where the time goes in v8:
time: 28.9 us; the launch traced here: 28.7 us
  blocking collectives  24.4 us (84%)
  Pallas kernels  3.63 us (13%)
  local copies, waits for them, and re-layouts  0.63 us (2%)
    all_to_all x1, blocking collectives, local(): lax.all_to_all(leaving, AXES, split_axis=0, concat_axis=0, tiled=True)  15.3 us
    all_to_all x1, blocking collectives, local(): lax.all_to_all(finished, AXES, split_axis=0, concat_axis=0, tiled=True)  9.11 us
    pallas_call x1, Pallas kernels, local(): pl.pallas_call(rows_kernel, out_shape=[jax.ShapeDtypeStruct((devices, loc...  2.07 us
    pallas_call x1, Pallas kernels, local(): pl.pallas_call(functools.partial(columns_kernel, local_v=local_v, views=v...  1.56 us
    unnamed x1, local copies, waits for them, and re-layouts  0.63 us

profile of v8, /device:TPU:0, one launch (start us, length us, event | category | flops | bytes accessed | tf_op | source)
XLA Modules:
  0.0 28.7 jit_solution(17015094495156168610)
XLA Ops:
  0.0 2.1 %rows.1 = (bf16[32,16,128]{2,1,0:T(8,128)(2,1)S(1)}, bf16[64,128]{1,0:T(8,128)(2,1)S(1)}, bf16[64,128]{1,0:T(8,128)(2,1)S(1)}, bf16[64,128]{1,0:T(8,128)(2,1)S(1...) custom-call(bf16[1,8,4,1024]{3,2,1,0:T(4,128)(2,1)} %x_hbm.1, ...), custom_call_target="tpu_custom_call" | custom-call | tf_op jit(solution)/shard_map/rows/pallas_call | solution.py:381
  2.1 15.3 %all_to_all.10.x_ref = bf16[32,16,128]{2,1,0:T(8,128)(2,1)S(1)} all-to-all(bf16[32,16,128]{2,1,0:T(8,128)(2,1)S(1)} %get-tuple-element.12), channel_id=1, replica_groups=mesh['line'=16,'view'=2] {'view','line'}, dimensions={0} | all-to-all | bytes 262144 | tf_op jit(solution)/shard_map/all_to_all | solution.py:402
  17.4 1.6 %columns.1 = bf16[64,4,128]{2,1,0:T(4,128)(2,1)S(1)} custom-call(bf16[32,16,128]{2,1,0:T(8,128)(2,1)S(1)} %all_to_all.10.x_ref, bf16[64,128]{1,0:T(8,128)(2,1)S(1)} %get-tuple-element.13.wq_ref, bf16[64,128]{1,0:T(8,128)(2,1)S(1)} %get-tuple-element.14.wk_ref, bf16[64,128]{1,0:T(8,128)(2,1)S(1)} %get-tuple-element.15.wv_ref, ...), custom_call_target="tpu_custom_call" | custom-call | tf_op jit(solution)/shard_map/columns/pallas_call | solution.py:403
  19.0 9.1 %all_to_all.11 = bf16[64,4,128]{2,1,0:T(4,128)(2,1)S(1)} all-to-all(bf16[64,4,128]{2,1,0:T(4,128)(2,1)S(1)} %columns.1), channel_id=1, replica_groups=mesh['line'=16,'view'=2] {'view','line'}, dimensions={0} | all-to-all | bytes 131072 | tf_op jit(solution)/shard_map/all_to_all | solution.py:413
  28.1 0.6 %copy.10 = bf16[1,8,4,1024]{3,2,1,0:T(4,128)(2,1)} copy(bf16[1,8,4,1024]{3,2,1,0:T(4,128)(2,1)S(1)} %bitcast.6) | data formatting | bytes 131072

commit v9 on v8

--- a/solution.py
+++ b/solution.py
@@ -60,8 +60,8 @@
 
 
 def blend(lines, values, scaling):
+    values = values()
     scores = [score(queries, keys, scaling) for queries, keys in lines]
-    values = values()
     weights = [soften(part) for part in scores]
     return [
         jnp.dot(part, weight, preferred_element_type=F32).astype(BF16)

time: 28.9 us -> 28.8 us (level)
  no operation moved by 1% of the time
where the time goes in v9:
time: 28.8 us; the launch traced here: 28.7 us
  blocking collectives  24.4 us (85%)
  Pallas kernels  3.57 us (12%)
  local copies, waits for them, and re-layouts  0.63 us (2%)
    all_to_all x1, blocking collectives, local(): lax.all_to_all(leaving, AXES, split_axis=0, concat_axis=0, tiled=True)  15.3 us
    all_to_all x1, blocking collectives, local(): lax.all_to_all(finished, AXES, split_axis=0, concat_axis=0, tiled=True)  9.1 us
    pallas_call x1, Pallas kernels, local(): pl.pallas_call(rows_kernel, out_shape=[jax.ShapeDtypeStruct((devices, loc...  2.04 us
    pallas_call x1, Pallas kernels, local(): pl.pallas_call(functools.partial(columns_kernel, local_v=local_v, views=v...  1.53 us
    unnamed x1, local copies, waits for them, and re-layouts  0.63 us

profile of v9, /device:TPU:0, one launch (start us, length us, event | category | flops | bytes accessed | tf_op | source)
XLA Modules:
  0.0 28.7 jit_solution(16753344207378508060)
XLA Ops:
  0.0 2.0 %rows.1 = (bf16[32,16,128]{2,1,0:T(8,128)(2,1)S(1)}, bf16[64,128]{1,0:T(8,128)(2,1)S(1)}, bf16[64,128]{1,0:T(8,128)(2,1)S(1)}, bf16[64,128]{1,0:T(8,128)(2,1)S(1...) custom-call(bf16[1,8,4,1024]{3,2,1,0:T(4,128)(2,1)} %x_hbm.1, ...), custom_call_target="tpu_custom_call" | custom-call | tf_op jit(solution)/shard_map/rows/pallas_call | solution.py:381
  2.0 15.3 %all_to_all.10.x_ref = bf16[32,16,128]{2,1,0:T(8,128)(2,1)S(1)} all-to-all(bf16[32,16,128]{2,1,0:T(8,128)(2,1)S(1)} %get-tuple-element.12), channel_id=1, replica_groups=mesh['line'=16,'view'=2] {'view','line'}, dimensions={0} | all-to-all | bytes 262144 | tf_op jit(solution)/shard_map/all_to_all | solution.py:402
  17.4 1.5 %columns.1 = bf16[64,4,128]{2,1,0:T(4,128)(2,1)S(1)} custom-call(bf16[32,16,128]{2,1,0:T(8,128)(2,1)S(1)} %all_to_all.10.x_ref, bf16[64,128]{1,0:T(8,128)(2,1)S(1)} %get-tuple-element.13.wq_ref, bf16[64,128]{1,0:T(8,128)(2,1)S(1)} %get-tuple-element.14.wk_ref, bf16[64,128]{1,0:T(8,128)(2,1)S(1)} %get-tuple-element.15.wv_ref, ...), custom_call_target="tpu_custom_call" | custom-call | tf_op jit(solution)/shard_map/columns/pallas_call | solution.py:403
  18.9 9.1 %all_to_all.11 = bf16[64,4,128]{2,1,0:T(4,128)(2,1)S(1)} all-to-all(bf16[64,4,128]{2,1,0:T(4,128)(2,1)S(1)} %columns.1), channel_id=1, replica_groups=mesh['line'=16,'view'=2] {'view','line'}, dimensions={0} | all-to-all | bytes 131072 | tf_op jit(solution)/shard_map/all_to_all | solution.py:413
  28.0 0.6 %copy.10 = bf16[1,8,4,1024]{3,2,1,0:T(4,128)(2,1)} copy(bf16[1,8,4,1024]{3,2,1,0:T(4,128)(2,1)S(1)} %bitcast.6) | data formatting | bytes 131072

commit v10 on v9

--- a/solution.py
+++ b/solution.py
@@ -13,6 +13,7 @@
 F32 = jnp.float32
 BF16 = jnp.bfloat16
 SUBLANES = 8
+PARTS = 1
 VMEM_BYTES = 16 * 1024 * 1024
 
 
@@ -354,6 +355,22 @@
         result = (images[step + 1].astype(F32) + value).astype(BF16)
         for source, slot in enumerate(slots):
             o_ref[source * own + step] = result[slot * local_v : (slot + 1) * local_v]
+
+
+def place_kernel(x_ref, o_hbm, departures):
+    share = x_ref.shape[0] // PARTS
+    copies = [
+        pltpu.make_async_copy(
+            x_ref.at[pl.ds(part * share, share)],
+            o_hbm.at[pl.ds(part * share, share)],
+            departures.at[part],
+        )
+        for part in range(PARTS)
+    ]
+    for copy in copies:
+        copy.start()
+    for copy in copies:
+        copy.wait()
 
 
 def local(light_field, query_weight, key_weight, value_weight, out_weight, conv_first, conv_second):
@@ -411,6 +428,15 @@
         name="columns",
     )(arrived, *later)
     returned = lax.all_to_all(finished, AXES, split_axis=0, concat_axis=0, tiled=True)
+    returned = pl.pallas_call(
+        place_kernel,
+        out_shape=jax.ShapeDtypeStruct(returned.shape, BF16),
+        in_specs=[pl.BlockSpec(memory_space=pltpu.VMEM)],
+        out_specs=pl.BlockSpec(memory_space=pltpu.HBM),
+        scratch_shapes=[pltpu.SemaphoreType.DMA((PARTS,))],
+        compiler_params=params,
+        name="place",
+    )(returned)
     result = returned.reshape(all_u, pairs, local_v, lanes).transpose(0, 2, 1, 3)
     return result.reshape(light_field.shape)
 

time: 28.8 us -> 28.8 us (level)
  Pallas kernels: 3.57 us -> 4.2 us
  local copies, waits for them, and re-layouts: 0.63 us -> 0 us
    pallas_call x0 -> x1, Pallas kernels: none -> 0.64 us  [local(): pl.pallas_call(place_kernel, out_shape=jax.ShapeDtypeStruct(returned.shap...]
    unnamed x1 -> x0, local copies, waits for them, and re-layouts: 0.63 us -> none
where the time goes in v10:
time: 28.8 us; the launch traced here: 28.7 us
  blocking collectives  24.4 us (85%)
  Pallas kernels  4.2 us (15%)
    all_to_all x1, blocking collectives, local(): lax.all_to_all(leaving, AXES, split_axis=0, concat_axis=0, tiled=True)  15.3 us
    all_to_all x1, blocking collectives, local(): lax.all_to_all(finished, AXES, split_axis=0, concat_axis=0, tiled=True)  9.1 us
    pallas_call x1, Pallas kernels, local(): pl.pallas_call(rows_kernel, out_shape=[jax.ShapeDtypeStruct((devices, loc...  2.04 us
    pallas_call x1, Pallas kernels, local(): pl.pallas_call(functools.partial(columns_kernel, local_v=local_v, views=v...  1.53 us
    pallas_call x1, Pallas kernels, local(): pl.pallas_call(place_kernel, out_shape=jax.ShapeDtypeStruct(returned.shap...  0.64 us

profile of v10, /device:TPU:0, one launch (start us, length us, event | category | flops | bytes accessed | tf_op | source)
XLA Modules:
  0.0 28.7 jit_solution(10770133411787909287)
XLA Ops:
  0.0 2.0 %rows.1 = (bf16[32,16,128]{2,1,0:T(8,128)(2,1)S(1)}, bf16[64,128]{1,0:T(8,128)(2,1)S(1)}, bf16[64,128]{1,0:T(8,128)(2,1)S(1)}, bf16[64,128]{1,0:T(8,128)(2,1)S(1...) custom-call(bf16[1,8,4,1024]{3,2,1,0:T(4,128)(2,1)} %x_hbm.1, ...), custom_call_target="tpu_custom_call" | custom-call | tf_op jit(solution)/shard_map/rows/pallas_call | solution.py:398
  2.0 15.3 %all_to_all.10.x_ref = bf16[32,16,128]{2,1,0:T(8,128)(2,1)S(1)} all-to-all(bf16[32,16,128]{2,1,0:T(8,128)(2,1)S(1)} %get-tuple-element.12), channel_id=1, replica_groups=mesh['line'=16,'view'=2] {'view','line'}, dimensions={0} | all-to-all | bytes 262144 | tf_op jit(solution)/shard_map/all_to_all | solution.py:419
  17.4 1.5 %columns.1 = bf16[64,4,128]{2,1,0:T(4,128)(2,1)S(1)} custom-call(bf16[32,16,128]{2,1,0:T(8,128)(2,1)S(1)} %all_to_all.10.x_ref, bf16[64,128]{1,0:T(8,128)(2,1)S(1)} %get-tuple-element.13.wq_ref, bf16[64,128]{1,0:T(8,128)(2,1)S(1)} %get-tuple-element.14.wk_ref, bf16[64,128]{1,0:T(8,128)(2,1)S(1)} %get-tuple-element.15.wv_ref, ...), custom_call_target="tpu_custom_call" | custom-call | tf_op jit(solution)/shard_map/columns/pallas_call | solution.py:420
  18.9 9.1 %all_to_all.11.x_ref = bf16[64,4,128]{2,1,0:T(4,128)(2,1)S(1)} all-to-all(bf16[64,4,128]{2,1,0:T(4,128)(2,1)S(1)} %columns.1), channel_id=1, replica_groups=mesh['line'=16,'view'=2] {'view','line'}, dimensions={0} | all-to-all | bytes 131072 | tf_op jit(solution)/shard_map/all_to_all | solution.py:430
  28.0 0.6 %place.1 = bf16[64,4,128]{2,1,0:T(4,128)(2,1)} custom-call(bf16[64,4,128]{2,1,0:T(4,128)(2,1)S(1)} %all_to_all.11.x_ref), custom_call_target="tpu_custom_call" | custom-call | tf_op jit(solution)/shard_map/place/pallas_call | solution.py:431
